TPU v7x, 32 devices: a whole 2x2x4 slice. The times are simulated.
32 devices in a mesh: lon: 16 (over z, x, core), lat: 2 (over y).
Axes of the slice: x: 2, y: 2, z: 4, core: 2. Of those that a mesh axis runs over, the one named last changes fastest.
Arguments:
- zonal_state: float32 [4, 32, 3, 8, 2048], P(None, None, None, 'lat', 'lon'), may hold values from -6 to 6
- zonal_courant: float32 [32, 8, 2048], P(None, 'lat', 'lon'), may hold values from -0.5 to 0.5
- zonal_length: int32 [8], P('lat'), may hold values from 512 to 2048, as said below
- zonal_owner: int32 [8, 2048], P('lat', 'lon'), may hold values from 0 to 63, as said below
- merid_state: float32 [4, 32, 3, 64, 256], P(None, None, None, 'lon', 'lat'), may hold values from -6 to 6
- merid_courant: float32 [32, 64, 256], P(None, 'lon', 'lat'), may hold values from -0.5 to 0.5
- mixing: float32 [4, 32, 32], replicated, may hold values from -0.18 to 0.18
Outputs:
- zonal_next: float32 [4, 32, 3, 8, 2048], P(None, None, None, 'lat', 'lon')
- merid_next: float32 [4, 32, 3, 64, 256], P(None, None, None, 'lon', 'lat')
- coupling: float32 [64, 8, 128], P('lon', 'lat')
Inputs may be any that keep to these rules, and one draw needn't show every extreme that they name: `zonal_owner`: non-decreasing along each row; each GCM column holds 16 to 48 consecutive cells of a row, and cell x belongs to a column g with |g - x // 32| <= 1. `zonal_length`: in each latitude sector (aligned blocks of 4 cycles) the first cycle holds 1088 cells and the second 2048.
All inputs are finite; a program needn't handle non-finite values.
Results may differ from a plain program's by a relative error of at most 0.0003.
Values sent between devices are 32-bit elements; how exact they have to be, the bound alone decides.
A program may use at most 64 MiB of HBM per device.

v0:
```python
import jax
import jax.numpy as jnp
from jax import lax
from jax.sharding import PartitionSpec as P

SUB = 4
CELLS_DEV = 128
GLON_DEV = 4


diffuse_along = 0.3
diffuse_across = 0.1


def padded_2(cells, sides, width, closed):
    for axis, dim in sides:
        count = lax.axis_size(axis)
        ends = count if closed else count - 1
        head = lax.slice_in_dim(cells, 0, width, axis=dim)
        tail = lax.slice_in_dim(cells, cells.shape[dim] - width, cells.shape[dim], axis=dim)
        cells = jnp.concatenate(
            [
                lax.ppermute(tail, axis, [(i, (i + 1) % count) for i in range(ends)]),
                cells,
                lax.ppermute(head, axis, [((i + 1) % count, i) for i in range(ends)]),
            ],
            axis=dim,
        )
    return cells


def from_behind(value, axis, steps):
    count = lax.axis_size(axis)
    pairs = [(source, (source + steps) % count) for source in range(count)]
    return lax.ppermute(value, axis, pairs)


def across_terms(field_now):
    plus_side = jnp.concatenate([field_now[:, :, 1:], field_now[:, :, 2:3]], axis=2)
    minus_side = jnp.concatenate([field_now[:, :, 0:1], field_now[:, :, :2]], axis=2)
    return diffuse_across * (plus_side + minus_side - 2.0 * field_now)


def tendency(field_now, forward_side, backward_side, courant, mixing):
    vertical = jnp.einsum("vkj,vjwrx->vkwrx", mixing, field_now, precision=lax.Precision.HIGHEST)
    advect = -0.5 * courant * (forward_side - backward_side)
    spread = diffuse_along * (forward_side - 2.0 * field_now + backward_side)
    return advect + spread + across_terms(field_now) + vertical


def cycle_ends(own_now, lon_index, own_tail):
    head_part = jnp.where(lon_index == 0, own_now[..., 0], 0.0)
    tail_part = jnp.sum(jnp.where(own_tail, own_now, 0.0), axis=-1)
    return lax.psum((head_part, tail_part), "lon")


def shards(
    zonal_state, zonal_courant, zonal_length, zonal_owner, merid_state, merid_courant, mixing
):
    rows_dev = zonal_state.shape[3]
    cells_dev = zonal_state.shape[4]
    lon_index = lax.axis_index("lon")
    lat_index = lax.axis_index("lat")
    lat_count = lax.axis_size("lat")
    cycle_total = cells_dev * lax.axis_size("lon")
    cells = lon_index * cells_dev + jnp.arange(cells_dev, dtype=jnp.int32)
    own_tail = cells[None, :] == zonal_length[:, None] - 1
    extended = jnp.mod(
        lon_index * cells_dev - SUB + jnp.arange(cells_dev + 2 * SUB, dtype=jnp.int32), cycle_total
    )
    at_tail = extended[None, :] == zonal_length[:, None] - 1
    at_head = extended[None, :] == 0
    active = extended[None, :] < zonal_length[:, None]
    zonal_now, courant_wide = (
        padded_2(zonal_state, (("lon", 4),), SUB, True),
        padded_2(zonal_courant[None, :, None], (("lon", 4),), SUB, True),
    )
    courant_wide = courant_wide[0]
    for substep in range(SUB):
        head_cell, tail_cell = cycle_ends(
            zonal_now[..., SUB : SUB + cells_dev], lon_index, own_tail
        )
        forward_side = jnp.concatenate([zonal_now[..., 1:], zonal_now[..., -1:]], axis=-1)
        backward_side = jnp.concatenate([zonal_now[..., :1], zonal_now[..., :-1]], axis=-1)
        forward_side = jnp.where(at_tail, head_cell[..., None], forward_side)
        backward_side = jnp.where(at_head, tail_cell[..., None], backward_side)
        change = tendency(zonal_now, forward_side, backward_side, courant_wide, mixing)
        zonal_now = jnp.where(active, zonal_now + change, zonal_now)
    zonal_now = zonal_now[..., SUB : SUB + cells_dev]
    merid_now = merid_state
    for substep in range(SUB):
        padded = padded_2(merid_now, (("lat", 4),), 1, False)
        north_edge, south_edge = from_behind(
            (merid_now[:, :, ::-1, :, -1], merid_now[:, :, ::-1, :, 0]),
            "lon",
            lax.axis_size("lon") // 2,
        )
        forward_side = padded[..., 2:]
        backward_side = padded[..., :-2]
        forward_side = forward_side.at[..., -1].set(
            jnp.where(lat_index == lat_count - 1, north_edge, forward_side[..., -1])
        )
        backward_side = backward_side.at[..., 0].set(
            jnp.where(lat_index == 0, south_edge, backward_side[..., 0])
        )
        merid_now = merid_now + tendency(
            merid_now, forward_side, backward_side, merid_courant[:, None], mixing
        )
    scale = GLON_DEV / (3.0 * CELLS_DEV)
    change_sum = jnp.sum(zonal_now - zonal_state, axis=2) * scale
    flat = change_sum.reshape(-1, rows_dev, cells_dev)
    nearby = lon_index * GLON_DEV - 1 + jnp.arange(GLON_DEV + 2, dtype=jnp.int32)
    near_table = (zonal_owner[:, :, None] == nearby[None, None, :]).astype(jnp.float32)
    near_terms = jnp.einsum("rxg,jrx->grj", near_table, flat, precision=lax.Precision.HIGHEST)
    widened = padded_2(near_terms, (("lon", 0),), 1, False)
    coupling = widened[2:-2]
    coupling = coupling.at[0].add(widened[0]).at[-1].add(widened[-1])
    return (zonal_now, merid_now, coupling)


def solution(mesh):
    return jax.shard_map(
        shards,
        mesh=mesh,
        in_specs=(
            P(None, None, None, "lat", "lon"),
            P(None, "lat", "lon"),
            P("lat"),
            P("lat", "lon"),
            P(None, None, None, "lon", "lat"),
            P(None, "lon", "lat"),
            P(),
        ),
        out_specs=(
            P(None, None, None, "lat", "lon"),
            P(None, None, None, "lon", "lat"),
            P("lon", "lat", None),
        ),
        check_vma=False,
    )
```

profile of v0, /device:TPU:0, one launch (start us, length us, event | category | flops | bytes accessed | tf_op | source)
XLA Modules:
  0.0 459.2 jit_solution(1524387161490078369)
XLA Ops:
  0.7 1.9 fusion.86
  4.8 2.6 collective-permute-start.2
  7.4 2.4 collective-permute-start.3
  13.5 5.8 %collective-permute-start.6 = (f32[4,32,3,4,1]{1,3,4,2,0:T(4,128)}, f32[4,32,3,4,1]{1,3,4,2,0:T(4,128)}, u32[]{:S(2)}, u32[]{:S(2)}) collective-permute-start(f32[4,32,3,4,1]{1,3,4,2,0:T(4,128)} %copy.1002), channel_id=1, source_target_pairs={{0,1},{2,3},{4,5},{6,7},{8,9},{10,11},{12,13},{14,15},{16,17},{18,... | collective-permute-start | bytes 18440 | tf_op jit(solution)/shard_map/ppermute | solution.py:23
  21.2 1.4 reverse_bitcast_fusion
  28.8 58.5 %all-reduce.3 = (f32[4,32,3,4]{1,3,2,0:T(4,128)}, f32[4,32,3,4]{1,3,2,0:T(4,128)}) all-reduce(f32[4,32,3,4]{1,3,2,0:T(4,128)} %get-tuple-element.279, f32[4,32,3,4]{1,3,2,0:T(4,128)S(1)} %fusion.28), channel_id=1, replica_groups=mesh['lon'=16,'lat'=2] {'lon'}, use_global_device_ids=true, to_apply=%region_2.3 | all-reduce | flops 3072 | bytes 24576 | tf_op jit(solution)/shard_map/psum | solution.py:54
  89.1 2.9 collective-permute-start.7
  94.7 1.4 fusion.55
  96.1 2.0 copy.967
  98.1 2.0 copy.962
  100.0 2.0 copy.965
  102.0 3.2 pad_maximum_fusion.8
  105.2 2.5 scatter.29
  107.7 4.4 scatter.26
  113.0 2.8 fusion.12
  121.5 4.8 %collective-permute-start.10 = (f32[4,32,3,4,1]{1,3,4,2,0:T(4,128)S(1)}, f32[4,32,3,4,1]{1,3,4,2,0:T(4,128)S(1)}, u32[]{:S(2)}, u32[]{:S(2)}) collective-permute-start(f32[4,32,3,4,1]{1,3,4,2,0:T(4,128)S(1)} %copy-done.25), channel_id=1, source_target_pairs={{0,1},{2,3},{4,5},{6,7},{8,9},{10,11},{12,13},{14,15},{16,17},{18,... | collective-permute-start | bytes 18440 | tf_op jit(solution)/shard_map/ppermute | solution.py:23
  126.4 2.5 collective-permute-start.9
  129.8 1.7 collective-permute-done.9
  131.8 2.1 collective-permute-done.11
  135.7 2.0 copy.976
  137.6 2.0 copy.979
  139.6 3.2 pad_maximum_fusion.6
  142.8 5.8 %scatter.30 = f32[4,32,3,4,128]{4,1,3,2,0:T(8,128)} dynamic-update-slice(f32[4,32,3,4,128]{4,1,3,2,0:T(8,128)} %get-tuple-element.263, f32[4,32,3,4,1]{4,1,3,2,0:T(8,128)S(1)} %copy.977, s32[]{:T(128)} %constant.268.clone.1, s32[]{:T(128)} %constant.268.clone.1, s32[]{:T(128)} %constant.268.clone.1, s32[]{:T(128)} %constant.268.clone.1, s32[]{:T(128)} %constant.278.clone.1) | dynamic-update-slice | bytes 12292 | tf_op jit(solution)/shard_map/scatter | solution.py:100
  148.6 2.3 scatter.31
  150.9 2.9 fusion.18
  160.1 4.5 collective-permute-start.14
  164.9 2.4 collective-permute-start.15
  167.7 2.0 collective-permute-done.15
  171.5 2.0 copy.982
  173.4 2.0 copy.985
  175.4 3.2 pad_maximum_fusion.4
  178.6 5.8 %scatter.34 = f32[4,32,3,4,128]{4,1,3,2,0:T(8,128)} dynamic-update-slice(f32[4,32,3,4,128]{4,1,3,2,0:T(8,128)} %get-tuple-element.255, f32[4,32,3,4,1]{4,1,3,2,0:T(8,128)S(1)} %copy.983, s32[]{:T(128)} %constant.268.clone.1, s32[]{:T(128)} %constant.268.clone.1, s32[]{:T(128)} %constant.268.clone.1, s32[]{:T(128)} %constant.268.clone.1, s32[]{:T(128)} %constant.278.clone.1) | dynamic-update-slice | bytes 12292 | tf_op jit(solution)/shard_map/scatter | solution.py:100
  184.4 2.3 scatter.35
  186.7 2.6 fusion.16
  195.7 2.3 collective-permute-start.17
  198.0 6.2 %collective-permute-start.18 = (f32[4,32,3,4,1]{1,3,4,2,0:T(4,128)}, f32[4,32,3,4,1]{1,3,4,2,0:T(4,128)}, u32[]{:S(2)}, u32[]{:S(2)}) collective-permute-start(f32[4,32,3,4,1]{1,3,4,2,0:T(4,128)} %copy.990), channel_id=1, source_target_pairs={{0,1},{2,3},{4,5},{6,7},{8,9},{10,11},{12,13},{14,15},{16,17},{18,... | collective-permute-start | bytes 18440 | tf_op jit(solution)/shard_map/ppermute | solution.py:23
  210.7 2.9 add_select_fusion.2
  213.6 1.8 fusion.27
  216.0 2.2 fusion.68
  218.2 1.6 fusion.70
  221.0 58.3 %all-reduce.2 = (f32[4,32,3,4]{1,3,2,0:T(4,128)}, f32[4,32,3,4]{1,3,2,0:T(4,128)}) all-reduce(f32[4,32,3,4]{1,3,2,0:T(4,128)S(1)} %fusion.26, f32[4,32,3,4]{1,3,2,0:T(4,128)S(1)} %get-tuple-element.232), channel_id=1, replica_groups=mesh['lon'=16,'lat'=2] {'lon'}, use_global_device_ids=true, to_apply=%region_5.6 | all-reduce | flops 3072 | bytes 24576 | tf_op jit(solution)/shard_map/psum | solution.py:54
  279.3 4.6 %add_select_fusion.1 = f32[4,32,3,4,136]{4,1,3,2,0:T(8,128)S(1)} fusion(f32[4,32,3,4,136]{4,1,3,2,0:T(8,128)S(1)} %add_select_fusion.2, f32[4,32,1,4,136]{4,1,3,2,0:T(8,128)} %get-tuple-element.238, f32[4,32,2,4,136]{4,1,3,2,0:T(8,128)} %get-tuple-element.240, f32[4,32,2,4,136]{4,1,3,2,0:T(8,128)} %get-tuple-element.239, ...), kind=kOutput, calls=%fused_computation.1 | convolution fusion | flops 84393984 | bytes 5113032 | tf_op jit(solution)/shard_map/vkj,vjwrx->vkwrx/dot_general | solution.py:45
  284.0 1.8 fusion.25
  286.3 2.2 fusion.65
  288.6 1.6 fusion.67
  291.3 58.6 %all-reduce.1 = (f32[4,32,3,4]{1,3,2,0:T(4,128)}, f32[4,32,3,4]{1,3,2,0:T(4,128)}) all-reduce(f32[4,32,3,4]{1,3,2,0:T(4,128)S(1)} %fusion.24, f32[4,32,3,4]{1,3,2,0:T(4,128)S(1)} %get-tuple-element.223), channel_id=1, replica_groups=mesh['lon'=16,'lat'=2] {'lon'}, use_global_device_ids=true, to_apply=%region_8.9 | all-reduce | flops 3072 | bytes 24576 | tf_op jit(solution)/shard_map/psum | solution.py:54
  349.9 4.6 %add_select_fusion = f32[4,32,3,4,136]{4,1,3,2,0:T(8,128)S(1)} fusion(f32[4,32,3,4,136]{4,1,3,2,0:T(8,128)S(1)} %add_select_fusion.1, f32[4,32,1,4,136]{4,1,3,2,0:T(8,128)} %get-tuple-element.229, f32[4,32,2,4,136]{4,1,3,2,0:T(8,128)} %get-tuple-element.231, f32[4,32,2,4,136]{4,1,3,2,0:T(8,128)} %get-tuple-element.230, ...), kind=kOutput, calls=%fused_computation | convolution fusion | flops 84393984 | bytes 5113032 | tf_op jit(solution)/shard_map/vkj,vjwrx->vkwrx/dot_general | solution.py:45
  354.5 1.6 fusion.64
  357.3 2.4 fusion.23
  360.9 1.7 fusion.62
  362.6 2.6 convolution_bitcast_fusion
  365.3 58.8 %all-reduce = (f32[4,32,3,4]{1,3,2,0:T(4,128)}, f32[4,32,3,4]{1,3,2,0:T(4,128)}) all-reduce(f32[4,32,3,4]{1,3,2,0:T(4,128)} %select_reduce_fusion, f32[4,32,3,4]{1,3,2,0:T(4,128)} %get-tuple-element.214), channel_id=1, replica_groups=mesh['lon'=16,'lat'=2] {'lon'}, use_global_device_ids=true, to_apply=%region_11.12 | all-reduce | flops 3072 | bytes 24576 | tf_op jit(solution)/shard_map/psum | solution.py:54
  424.1 2.3 maximum_add_fusion.3
  426.9 1.4 fusion.19
  428.6 2.2 subtract_reduce_fusion
  432.4 1.8 collective-permute-start.20
  434.2 1.5 collective-permute-start.21
  438.0 2.0 copy.988
  440.0 2.0 copy.991
  441.9 2.9 pad_maximum_fusion.2
  444.9 5.8 %scatter.36 = f32[4,32,3,4,128]{4,1,3,2,0:T(8,128)} dynamic-update-slice(f32[4,32,3,4,128]{4,1,3,2,0:T(8,128)} %get-tuple-element.247, f32[4,32,3,4,1]{4,1,3,2,0:T(8,128)S(1)} %copy.989, s32[]{:T(128)} %constant.268.clone.1, s32[]{:T(128)} %constant.268.clone.1, s32[]{:T(128)} %constant.268.clone.1, s32[]{:T(128)} %constant.268.clone.1, s32[]{:T(128)} %constant.278.clone.1) | dynamic-update-slice | bytes 12292 | tf_op jit(solution)/shard_map/scatter | solution.py:100
  451.8 2.4 fusion.14
  454.2 1.4 copy.996
  455.6 1.4 copy.995
  (191 shorter events, 62.9 us)
Async XLA Ops:
  0.6 112.4 %copy-start = (f32[4,32,32]{2,1,0:T(8,128)S(1)}, f32[4,32,32]{2,1,0:T(8,128)}, u32[]{:S(2)}) copy-start(f32[4,32,32]{2,1,0:T(8,128)} %param.33) | copy-start | bytes 49156
  0.6 3.5 copy-start.15
  0.7 9.1 %copy-start.3 = (f32[4,32,3,4,128]{4,3,2,1,0:T(4,128)S(1)}, f32[4,32,3,4,128]{4,3,2,1,0:T(4,128)}, u32[]{:S(2)}) copy-start(f32[4,32,3,4,128]{4,3,2,1,0:T(4,128)} %param.31) | copy-start | bytes 2359300
  3.6 201.5 %collective-permute-start = (f32[4,32,3,4,4]{1,4,3,2,0:T(4,128)}, f32[4,32,3,4,4]{1,4,3,2,0:T(4,128)}, u32[]{:S(2)}, u32[]{:S(2)}) collective-permute-start(f32[4,32,3,4,4]{1,4,3,2,0:T(4,128)} %copy.999), channel_id=1, source_target_pairs={{0,2},{2,4},{4,6},{6,8},{8,10},{10,12},{12,14},{14,16},{16,18},{18... | collective-permute-start | bytes 73736 | tf_op jit(solution)/shard_map/ppermute | solution.py:23
  4.8 82.4 %collective-permute-start.2 = (f32[1,32,1,4,4]{4,3,1,2,0:T(4,128)}, f32[1,32,1,4,4]{4,3,1,2,0:T(4,128)}, u32[]{:S(2)}, u32[]{:S(2)}) collective-permute-start(f32[1,32,1,4,4]{4,3,1,2,0:T(4,128)} %get-tuple-element.283), channel_id=1, source_target_pairs={{0,2},{2,4},{4,6},{6,8},{8,10},{10,12},{12,14},{14,16},{16,18},{18... | collective-permute-start | bytes 6152 | tf_op jit(solution)/shard_map/ppermute | solution.py:23
  7.4 79.8 %collective-permute-start.3 = (f32[1,32,1,4,4]{4,3,1,2,0:T(4,128)}, f32[1,32,1,4,4]{4,3,1,2,0:T(4,128)}, u32[]{:S(2)}, u32[]{:S(2)}) collective-permute-start(f32[1,32,1,4,4]{4,3,1,2,0:T(4,128)} %get-tuple-element.284), channel_id=1, source_target_pairs={{2,0},{4,2},{6,4},{8,6},{10,8},{12,10},{14,12},{16,14},{18,16},{20... | collective-permute-start | bytes 6152 | tf_op jit(solution)/shard_map/ppermute | solution.py:25
  11.3 77.9 %collective-permute-start.4 = (f32[4,32,3,4,1]{1,3,4,2,0:T(4,128)}, f32[4,32,3,4,1]{1,3,4,2,0:T(4,128)}, u32[]{:S(2)}, u32[]{:S(2)}) collective-permute-start(f32[4,32,3,4,1]{1,3,4,2,0:T(4,128)} %copy.1001), channel_id=1, source_target_pairs={{1,0},{3,2},{5,4},{7,6},{9,8},{11,10},{13,12},{15,14},{17,16},{19,... | collective-permute-start | bytes 18440 | tf_op jit(solution)/shard_map/ppermute | solution.py:25
  13.5 81.2 %collective-permute-start.6 = (f32[4,32,3,4,1]{1,3,4,2,0:T(4,128)}, f32[4,32,3,4,1]{1,3,4,2,0:T(4,128)}, u32[]{:S(2)}, u32[]{:S(2)}) collective-permute-start(f32[4,32,3,4,1]{1,3,4,2,0:T(4,128)} %copy.1002), channel_id=1, source_target_pairs={{0,1},{2,3},{4,5},{6,7},{8,9},{10,11},{12,13},{14,15},{16,17},{18,... | collective-permute-start | bytes 18440 | tf_op jit(solution)/shard_map/ppermute | solution.py:23
  22.6 1.9 copy-start.34
  22.6 1.9 copy-start.4
  23.7 4.7 %copy-start.23 = (f32[32,4,128]{2,1,0:T(4,128)S(1)}, f32[32,4,128]{2,1,0:T(4,128)}, u32[]{:S(2)}) copy-start(f32[32,4,128]{2,1,0:T(4,128)} %param.32) | copy-start | bytes 196612
  24.5 1.0 copy-start.35
  87.2 119.8 %collective-permute-start.1 = (f32[4,32,3,4,4]{1,4,3,2,0:T(4,128)}, f32[4,32,3,4,4]{1,4,3,2,0:T(4,128)}, u32[]{:S(2)}, u32[]{:S(2)}) collective-permute-start(f32[4,32,3,4,4]{1,4,3,2,0:T(4,128)} %copy.1000), channel_id=1, source_target_pairs={{2,0},{4,2},{6,4},{8,6},{10,8},{12,10},{14,12},{16,14},{18,16},{20... | collective-permute-start | bytes 73736 | tf_op jit(solution)/shard_map/ppermute | solution.py:25
  87.2 5.0 %collective-permute-start.5 = (f32[4,32,3,4]{1,3,2,0:T(4,128)}, f32[4,32,3,4]{1,3,2,0:T(4,128)S(1)}, u32[]{:S(2)}, u32[]{:S(2)}) collective-permute-start(f32[4,32,3,4]{1,3,2,0:T(4,128)} %reverse_bitcast_fusion.1), channel_id=1, source_target_pairs={{0,16},{2,18},{4,20},{6,22},{8,24},{10,26},{12,28},{14,30},{16,0},... | collective-permute-start | bytes 18440 | tf_op jit(solution)/shard_map/ppermute | solution.py:35
  88.4 3.8 copy-start.16
  89.1 5.5 %collective-permute-start.7 = (f32[4,32,3,4]{1,3,2,0:T(4,128)}, f32[4,32,3,4]{1,3,2,0:T(4,128)}, u32[]{:S(2)}, u32[]{:S(2)}) collective-permute-start(f32[4,32,3,4]{1,3,2,0:T(4,128)} %reverse_bitcast_fusion), channel_id=1, source_target_pairs={{0,16},{2,18},{4,20},{6,22},{8,24},{10,26},{12,28},{14,30},{16,0},... | collective-permute-start | bytes 18440 | tf_op jit(solution)/shard_map/ppermute | solution.py:35
  105.2 2.5 copy-start.10
  112.1 0.9 copy-start.11
  118.0 3.5 copy-start.25
  118.0 8.4 %copy-start.28 = (f32[4,32,3,4]{1,3,2,0:T(4,128)S(1)}, f32[4,32,3,4]{1,3,2,0:T(4,128)}, u32[]{:S(2)}) copy-start(f32[4,32,3,4]{1,3,2,0:T(4,128)} %reverse_reduce_fusion.5) | copy-start | bytes 18436
  120.2 8.9 %collective-permute-start.8 = (f32[4,32,3,4,1]{1,3,4,2,0:T(4,128)S(1)}, f32[4,32,3,4,1]{1,3,4,2,0:T(4,128)S(1)}, u32[]{:S(2)}, u32[]{:S(2)}) collective-permute-start(f32[4,32,3,4,1]{1,3,4,2,0:T(4,128)S(1)} %copy.975), channel_id=1, source_target_pairs={{1,0},{3,2},{5,4},{7,6},{9,8},{11,10},{13,12},{15,14},{17,16},{19,... | collective-permute-start | bytes 18440 | tf_op jit(solution)/shard_map/ppermute | solution.py:25
  121.5 10.3 %collective-permute-start.10 = (f32[4,32,3,4,1]{1,3,4,2,0:T(4,128)S(1)}, f32[4,32,3,4,1]{1,3,4,2,0:T(4,128)S(1)}, u32[]{:S(2)}, u32[]{:S(2)}) collective-permute-start(f32[4,32,3,4,1]{1,3,4,2,0:T(4,128)S(1)} %copy-done.25), channel_id=1, source_target_pairs={{0,1},{2,3},{4,5},{6,7},{8,9},{10,11},{12,13},{14,15},{16,17},{18,... | collective-permute-start | bytes 18440 | tf_op jit(solution)/shard_map/ppermute | solution.py:23
  126.4 5.0 %collective-permute-start.9 = (f32[4,32,3,4]{1,3,2,0:T(4,128)S(1)}, f32[4,32,3,4]{1,3,2,0:T(4,128)S(1)}, u32[]{:S(2)}, u32[]{:S(2)}) collective-permute-start(f32[4,32,3,4]{1,3,2,0:T(4,128)S(1)} %copy-done.28), channel_id=1, source_target_pairs={{0,16},{2,18},{4,20},{6,22},{8,24},{10,26},{12,28},{14,30},{16,0},... | collective-permute-start | bytes 18440 | tf_op jit(solution)/shard_map/ppermute | solution.py:35
  129.1 4.8 %copy-start.19 = (f32[4,32,3,4,1]{1,3,4,2,0:T(4,128)}, f32[4,32,3,4,1]{1,3,4,2,0:T(4,128)S(1)}, u32[]{:S(2)}) copy-start(f32[4,32,3,4,1]{1,3,4,2,0:T(4,128)S(1)} %collective-permute-done.8) | copy-start | bytes 18436
  129.2 4.8 %collective-permute-start.11 = (f32[4,32,3,4]{1,3,2,0:T(4,128)S(1)}, f32[4,32,3,4]{1,3,2,0:T(4,128)S(1)}, u32[]{:S(2)}, u32[]{:S(2)}) collective-permute-start(f32[4,32,3,4]{1,3,2,0:T(4,128)S(1)} %reverse_reduce_fusion.4), channel_id=1, source_target_pairs={{0,16},{2,18},{4,20},{6,22},{8,24},{10,26},{12,28},{14,30},{16,0},... | collective-permute-start | bytes 18440 | tf_op jit(solution)/shard_map/ppermute | solution.py:35
  131.8 2.2 copy-start.21
  155.9 3.5 copy-start.27
  155.9 4.2 copy-start.26
  158.1 6.8 %collective-permute-start.12 = (f32[4,32,3,4,1]{1,3,4,2,0:T(4,128)S(1)}, f32[4,32,3,4,1]{1,3,4,2,0:T(4,128)S(1)}, u32[]{:S(2)}, u32[]{:S(2)}) collective-permute-start(f32[4,32,3,4,1]{1,3,4,2,0:T(4,128)S(1)} %copy.981), channel_id=1, source_target_pairs={{1,0},{3,2},{5,4},{7,6},{9,8},{11,10},{13,12},{15,14},{17,16},{19,... | collective-permute-start | bytes 18440 | tf_op jit(solution)/shard_map/ppermute | solution.py:25
  159.4 7.9 %collective-permute-start.13 = (f32[4,32,3,4]{1,3,2,0:T(4,128)S(1)}, f32[4,32,3,4]{1,3,2,0:T(4,128)S(1)}, u32[]{:S(2)}, u32[]{:S(2)}) collective-permute-start(f32[4,32,3,4]{1,3,2,0:T(4,128)S(1)} %copy-done.27), channel_id=1, source_target_pairs={{0,16},{2,18},{4,20},{6,22},{8,24},{10,26},{12,28},{14,30},{16,0},... | collective-permute-start | bytes 18440 | tf_op jit(solution)/shard_map/ppermute | solution.py:35
  160.1 7.6 %collective-permute-start.14 = (f32[4,32,3,4,1]{1,3,4,2,0:T(4,128)S(1)}, f32[4,32,3,4,1]{1,3,4,2,0:T(4,128)S(1)}, u32[]{:S(2)}, u32[]{:S(2)}) collective-permute-start(f32[4,32,3,4,1]{1,3,4,2,0:T(4,128)S(1)} %copy-done.26), channel_id=1, source_target_pairs={{0,1},{2,3},{4,5},{6,7},{8,9},{10,11},{12,13},{14,15},{16,17},{18,... | collective-permute-start | bytes 18440 | tf_op jit(solution)/shard_map/ppermute | solution.py:23
  164.9 4.8 %copy-start.20 = (f32[4,32,3,4,1]{1,3,4,2,0:T(4,128)}, f32[4,32,3,4,1]{1,3,4,2,0:T(4,128)S(1)}, u32[]{:S(2)}) copy-start(f32[4,32,3,4,1]{1,3,4,2,0:T(4,128)S(1)} %collective-permute-done.12) | copy-start | bytes 18436
  164.9 4.8 %collective-permute-start.15 = (f32[4,32,3,4]{1,3,2,0:T(4,128)S(1)}, f32[4,32,3,4]{1,3,2,0:T(4,128)S(1)}, u32[]{:S(2)}, u32[]{:S(2)}) collective-permute-start(f32[4,32,3,4]{1,3,2,0:T(4,128)S(1)} %reverse_reduce_fusion.2), channel_id=1, source_target_pairs={{0,16},{2,18},{4,20},{6,22},{8,24},{10,26},{12,28},{14,30},{16,0},... | collective-permute-start | bytes 18440 | tf_op jit(solution)/shard_map/ppermute | solution.py:35
  167.7 2.0 copy-start.22
  184.4 2.4 copy-start.13
  189.4 1.4 copy-start.1
  192.5 241.7 %collective-permute-start.16 = (f32[4,32,3,4,1]{1,3,4,2,0:T(4,128)}, f32[4,32,3,4,1]{1,3,4,2,0:T(4,128)}, u32[]{:S(2)}, u32[]{:S(2)}) collective-permute-start(f32[4,32,3,4,1]{1,3,4,2,0:T(4,128)} %copy.987), channel_id=1, source_target_pairs={{1,0},{3,2},{5,4},{7,6},{9,8},{11,10},{13,12},{15,14},{17,16},{19,... | collective-permute-start | bytes 18440 | tf_op jit(solution)/shard_map/ppermute | solution.py:25
  195.7 240.0 %collective-permute-start.17 = (f32[4,32,3,4]{1,3,2,0:T(4,128)}, f32[4,32,3,4]{1,3,2,0:T(4,128)}, u32[]{:S(2)}, u32[]{:S(2)}) collective-permute-start(f32[4,32,3,4]{1,3,2,0:T(4,128)} %reverse_reduce_fusion.1), channel_id=1, source_target_pairs={{0,16},{2,18},{4,20},{6,22},{8,24},{10,26},{12,28},{14,30},{16,0},... | collective-permute-start | bytes 18440 | tf_op jit(solution)/shard_map/ppermute | solution.py:35
  198.0 238.8 %collective-permute-start.18 = (f32[4,32,3,4,1]{1,3,4,2,0:T(4,128)}, f32[4,32,3,4,1]{1,3,4,2,0:T(4,128)}, u32[]{:S(2)}, u32[]{:S(2)}) collective-permute-start(f32[4,32,3,4,1]{1,3,4,2,0:T(4,128)} %copy.990), channel_id=1, source_target_pairs={{0,1},{2,3},{4,5},{6,7},{8,9},{10,11},{12,13},{14,15},{16,17},{18,... | collective-permute-start | bytes 18440 | tf_op jit(solution)/shard_map/ppermute | solution.py:23
  205.1 231.7 %collective-permute-start.19 = (f32[4,32,3,4]{1,3,2,0:T(4,128)}, f32[4,32,3,4]{1,3,2,0:T(4,128)}, u32[]{:S(2)}, u32[]{:S(2)}) collective-permute-start(f32[4,32,3,4]{1,3,2,0:T(4,128)} %reverse_reduce_fusion), channel_id=1, source_target_pairs={{0,16},{2,18},{4,20},{6,22},{8,24},{10,26},{12,28},{14,30},{16,0},... | collective-permute-start | bytes 18440 | tf_op jit(solution)/shard_map/ppermute | solution.py:35
  209.8 0.9 copy-start.17
  209.8 0.9 copy-start.32
  209.8 0.9 copy-start.37
  209.8 0.9 copy-start.38
  424.1 2.4 copy-start.6
  424.1 2.5 copy-start.8
  424.1 2.8 copy-start.9
  424.1 2.8 copy-start.29
  424.1 2.8 copy-start.30
  426.9 1.4 copy-start.5
  426.9 1.7 copy-start.7
  426.9 1.7 copy-start.18
  426.9 1.6 copy-start.36
  428.6 2.3 copy-start.31
  428.6 2.3 copy-start.33
  432.4 24.6 %collective-permute-start.20 = (f32[1,4,128]{2,0,1:T(1,128)}, f32[1,4,128]{2,0,1:T(1,128)}, u32[]{:S(2)}, u32[]{:S(2)}) collective-permute-start(f32[1,4,128]{2,0,1:T(1,128)} %get-tuple-element.286), channel_id=1, source_target_pairs={{0,2},{2,4},{4,6},{6,8},{8,10},{10,12},{12,14},{14,16},{16,18},{18... | collective-permute-start | bytes 6152 | tf_op jit(solution)/shard_map/ppermute | solution.py:23
  434.2 23.5 %collective-permute-start.21 = (f32[1,4,128]{2,0,1:T(1,128)}, f32[1,4,128]{2,0,1:T(1,128)}, u32[]{:S(2)}, u32[]{:S(2)}) collective-permute-start(f32[1,4,128]{2,0,1:T(1,128)} %get-tuple-element.285), channel_id=1, source_target_pairs={{2,0},{4,2},{6,4},{8,6},{10,8},{12,10},{14,12},{16,14},{18,16},{20... | collective-permute-start | bytes 6152 | tf_op jit(solution)/shard_map/ppermute | solution.py:25
  436.5 5.5 %copy-start.2 = (f32[4,32,3,4,128]{4,1,3,2,0:T(8,128)S(1)}, f32[4,32,3,4,128]{4,1,3,2,0:T(8,128)}, u32[]{:S(2)}) copy-start(f32[4,32,3,4,128]{4,1,3,2,0:T(8,128)} %copy-done.1) | copy-start | bytes 2359300
  450.6 1.1 copy-start.12
  454.2 1.4 copy-start.14
  454.2 3.4 copy-start.24
where the time goes:
time: 468 us; the launch traced here: 459 us
  blocking collectives  234 us (50%)
  local copies, waits for them, and re-layouts  106 us (23%)
  starting transfers between devices  47.3 us (10%)
  other arithmetic  38.5 us (8%)
  matrix products  25.9 us (6%)
  waiting for transfers between devices  6.03 us (1%)
    psum x4, blocking collectives, cycle_ends(): return lax.psum((head_part, tail_part), 'lon')  234 us
    ppermute x7, starting transfers between devices, padded_2(): lax.ppermute(tail, axis, [(i, (i + 1) % count) for i in range(ends)])  26.2 us
    dot_general x8, matrix products, tendency(): jnp.einsum('vkj,vjwrx->vkwrx', mixing, field_now, precision=lax.Precision...  25.6 us
    scatter x4, local copies, waits for them, and re-layouts, shards(): forward_side.at[..., -1]  21.8 us
    concatenate x5, other arithmetic, padded_2(): jnp.concatenate([lax.ppermute(tail, axis, [(i, (i + 1) % count) for i in...  13.2 us
    ppermute x8, starting transfers between devices, from_behind(): return lax.ppermute(value, axis, pairs)  12 us
    unnamed x86, local copies, waits for them, and re-layouts  9.74 us
    slice x8, local copies, waits for them, and re-layouts, across_terms(): field_now[:, :, :2]  9.51 us
  transfers between devices with their start and end apart: 22, of which 4 were waited for; matrix products, arithmetic and copies ran while one was open for 36% of the time, Pallas kernels for 0%

commit v1 on v0

v1 whole, which is shorter than its diff:
```python
import functools

import jax
import jax.numpy as jnp
from jax import lax
from jax.experimental import pallas as pl
from jax.experimental.pallas import tpu as pltpu
from jax.sharding import PartitionSpec as P

SUB = 4
GLON_DEV = 4
PAD = 8
MESH = pl.DeviceIdType.MESH
F32 = jnp.float32


def mix_into(products, at, fields, weights):
    wide = jnp.concatenate(fields, axis=0)
    high = wide.astype(jnp.bfloat16)
    low = (wide - high.astype(F32)).astype(jnp.bfloat16)
    out = jnp.dot(jnp.concatenate([high, low], axis=1), weights[...], preferred_element_type=F32)
    half = out.shape[1] // 2
    products[pl.ds(at, wide.shape[0]), :] = out[:, :half] + out[:, half:]


def updated(now, ahead, behind, courant, product):
    c_ahead = 0.3 - 0.5 * courant
    c_behind = 0.3 + 0.5 * courant
    x0, x1, x2 = now
    local = (0.3 * x0 + 0.1 * x1, 0.2 * x1 + 0.1 * (x0 + x2), 0.3 * x2 + 0.1 * x1)
    return [
        local[w] + c_ahead * ahead[w] + c_behind * behind[w] + product[w] for w in range(3)
    ]


def substep(state, strips, products, weights, src, dst, cells, rows_dev, tails, strips_too):
    rows = 3 * cells
    for r in range(rows_dev):
        mix_into(
            products,
            r * rows,
            [state[src, w * 4 + r, pl.ds(PAD, cells), :] for w in range(3)],
            weights,
        )
    srows = 16 * rows_dev
    if strips_too:
        mix_into(
            products,
            rows_dev * rows,
            [strips[src, w, pl.ds(PAD, srows), :] for w in range(3)],
            weights,
        )
    for r in range(rows_dev):
        for w in range(3):
            edge = PAD + r * 16 + 3
            state[src, w * 4 + r, pl.ds(PAD - 1, 1), :] = strips[src, w, pl.ds(edge, 1), :]
            state[src, w * 4 + r, pl.ds(PAD + cells, 1), :] = strips[src, w, pl.ds(edge + 8, 1), :]
    step = 32
    for r in range(rows_dev):
        for at in range(0, cells, step):
            now = [state[src, w * 4 + r, pl.ds(PAD + at, step), :] for w in range(3)]
            ahead = [state[src, w * 4 + r, pl.ds(PAD + at + 1, step), :] for w in range(3)]
            behind = [state[src, w * 4 + r, pl.ds(PAD + at - 1, step), :] for w in range(3)]
            courant = state[0, 12 + r, pl.ds(PAD + at, step), :]
            product = [
                products[pl.ds(r * rows + w * cells + at, step), :] for w in range(3)
            ]
            if tails is not None:
                index = at + lax.broadcasted_iota(jnp.int32, (step, 128), 0)
                end = tails[r]
                for w in range(3):
                    beyond = strips[src, w, pl.ds(PAD + r * 16 + 11, 1), :]
                    ahead[w] = jnp.where(index == end - 1, beyond, ahead[w])
            new = updated(now, ahead, behind, courant, product)
            for w in range(3):
                value = new[w]
                if tails is not None:
                    value = jnp.where(index < end, value, now[w])
                state[dst, w * 4 + r, pl.ds(PAD + at, step), :] = value
    if strips_too:
        base = rows_dev * rows
        for at in range(0, srows, step):
            now = [strips[src, w, pl.ds(PAD + at, step), :] for w in range(3)]
            ahead = [strips[src, w, pl.ds(PAD + at + 1, step), :] for w in range(3)]
            behind = [strips[src, w, pl.ds(PAD + at - 1, step), :] for w in range(3)]
            courant = strips[0, 3, pl.ds(PAD + at, step), :]
            product = [products[pl.ds(base + w * srows + at, step), :] for w in range(3)]
            new = updated(now, ahead, behind, courant, product)
            for w in range(3):
                strips[dst, w, pl.ds(PAD + at, step), :] = new[w]


def load_state(state, field, courant, cells, rows_dev):
    for r in range(rows_dev):
        for w in range(3):
            at = w * rows_dev + r
            block = field[pl.ds(at, 128, stride=3 * rows_dev), :]
            state[0, w * 4 + r, pl.ds(PAD, cells), :] = block.T
        levels = courant[pl.ds(r, 32, stride=rows_dev), :]
        state[0, 12 + r, pl.ds(PAD, cells), :] = jnp.concatenate([levels] * 4, axis=0).T


def store_state(out, state, cells, rows_dev):
    for r in range(rows_dev):
        for w in range(3):
            at = w * rows_dev + r
            out[pl.ds(at, 128, stride=3 * rows_dev), :] = state[0, w * 4 + r, pl.ds(PAD, cells), :].T


def pack_ends(first, last, state, cells, rows_dev):
    for r in range(rows_dev):
        for ch in range(4):
            put = pl.ds((r % 2) * 4, 4)
            first[r // 2, ch, put, :] = state[0, ch * 4 + r, pl.ds(PAD, 4), :]
            last[r // 2, ch, put, :] = state[0, ch * 4 + r, pl.ds(PAD + cells - 4, 4), :]


def kernel(
    n, n_lat, cells, rows_dev,
    len_ref, z_ref, zc_ref, own_ref, m_ref, mc_ref, mix_ref,
    zo_ref, mo_ref, co_ref,
    zs, ms, zh, mh, products, weights, start_sum,
    z_first, z_last, z_tail, m_first, m_last,
    from_left, from_right, heads, tails_in, tail_zero, m_halo, head_rows,
    c_left, c_right, c_from_left, c_from_right,
    sends, recvs, tail_sends, tail_recvs, head_sends,
):
    me = lax.axis_index("lon")
    lat = lax.axis_index("lat")
    right, left = lax.rem(me + 1, n), lax.rem(me + n - 1, n)
    partner = lax.rem(me + n // 2, n)
    wrap_from = n // 4 - 1
    mid = n // 2
    start = me * cells
    barrier = pltpu.get_barrier_semaphore()

    def greet(lon_to, lat_to):
        pl.semaphore_signal(barrier, inc=1, device_id=(lon_to, lat_to), device_id_type=MESH)

    greet(left, lat)
    greet(right, lat)
    at_south, at_north = lat == 0, lat == n_lat - 1
    south_lon = jnp.where(at_south, partner, me)
    south_lat = jnp.where(at_south, 0, lat - 1)
    north_lon = jnp.where(at_north, partner, me)
    north_lat = jnp.where(at_north, n_lat - 1, lat + 1)
    greet(south_lon, south_lat)
    greet(north_lon, north_lat)

    @pl.when(me == 0)
    def _():
        for j in range(wrap_from, n):
            greet(j, lat)

    @pl.when(me >= wrap_from)
    def _():
        greet(0, lat)

    load_state(zs, z_ref, zc_ref, cells, rows_dev)
    pack_ends(z_first, z_last, zs, cells, rows_dev)
    lengths = [len_ref[r] for r in range(rows_dev)]
    index8 = lax.broadcasted_iota(jnp.int32, (8, 128), 0)
    for r in range(rows_dev):
        at = jnp.clip(lengths[r] - 4 - start, -4, cells)
        cell = lengths[r] - 4 - start + index8
        own = (cell >= 0) & (cell < cells)
        for ch in range(4):
            value = zs[0, ch * 4 + r, pl.ds(PAD + at, 8), :]
            z_tail[r // 2, ch, pl.ds((r % 2) * 4, 4), :] = jnp.where(own, value, 0.0)[:4]
    load_state(ms, m_ref, mc_ref, cells, rows_dev)
    pack_ends(m_first, m_last, ms, cells, rows_dev)

    extra = jnp.where(me == 0, n - wrap_from, jnp.where(me >= wrap_from, 1, 0))
    pl.semaphore_wait(barrier, 4 + extra)

    def copy(src, dst, send, recv, lon_to, lat_to):
        return pltpu.make_async_remote_copy(
            src_ref=src, dst_ref=dst, send_sem=send, recv_sem=recv,
            device_id=(lon_to, lat_to), device_id_type=MESH,
        )

    def head_copy(j):
        return copy(z_first.at[1], heads.at[1], head_sends.at[j], recvs.at[4], j, lat)

    head_mid = copy(z_first.at[0], heads.at[0], sends.at[5], recvs.at[5], mid, lat)
    tail_mid = copy(z_tail.at[0], tail_zero, sends.at[5], recvs.at[6], 0, lat)

    def tail_copy(j):
        return copy(z_tail.at[1], tails_in.at[j], sends.at[4], tail_recvs.at[j], 0, lat)

    @pl.when(me == 0)
    def _():
        for j in range(wrap_from, n):
            head_copy(j).start()
        head_mid.start()

    @pl.when(me >= wrap_from)
    def _():
        tail_copy(me).start()

    @pl.when(me == mid)
    def _():
        tail_mid.start()

    to_right = copy(z_last, from_left, sends.at[0], recvs.at[0], right, lat)
    to_left = copy(z_first, from_right, sends.at[1], recvs.at[1], left, lat)
    to_right.start()
    to_left.start()
    south_slot = jnp.where(at_south, 0, 1)
    north_slot = jnp.where(at_north, 1, 0)
    to_south = copy(
        m_first, m_halo.at[south_slot], sends.at[2], recvs.at[2 + south_slot], south_lon, south_lat
    )
    to_north = copy(
        m_last, m_halo.at[north_slot], sends.at[3], recvs.at[2 + north_slot], north_lon, north_lat
    )
    to_south.start()
    to_north.start()

    tiled = jnp.concatenate([mix_ref[...]] * 4, axis=1)
    block_of = lambda axis: lax.broadcasted_iota(jnp.int32, (128, 128), axis) // 32
    matrix = jnp.where(block_of(0) == block_of(1), tiled, 0.0).T
    w_high = matrix.astype(jnp.bfloat16)
    w_low = (matrix - w_high.astype(F32)).astype(jnp.bfloat16)
    pair = jnp.concatenate([w_high, w_low], axis=1)
    weights[pl.ds(0, 128), :] = pair
    weights[pl.ds(128, 128), :] = pair
    for r in range(rows_dev):
        body = pl.ds(PAD, cells)
        start_sum[r] = zs[0, r, body, :] + zs[0, 4 + r, body, :] + zs[0, 8 + r, body, :]
    for buf in (zh, mh):
        for s in range(2):
            for ch in range(4):
                buf[s, ch, pl.ds(0, 8), :] = jnp.zeros((8, 128), F32)
                buf[s, ch, pl.ds(PAD + 16 * rows_dev, 8), :] = jnp.zeros((8, 128), F32)

    to_right.wait()
    to_left.wait()

    @pl.when(me >= wrap_from)
    def _():
        tail_copy(me).wait_send()
        head_copy(me).wait_recv()

    @pl.when(me == mid)
    def _():
        tail_mid.wait_send()
        head_mid.wait_recv()

    @pl.when(me == 0)
    def _():
        for j in range(wrap_from, n):
            head_copy(j).wait_send()
            tail_copy(j).wait_recv()
        head_mid.wait_send()
        tail_mid.wait_recv()

    for r in range(rows_dev):
        take = pl.ds((r % 2) * 4, 4)
        for ch in range(4):
            zs[0, ch * 4 + r, pl.ds(PAD - 4, 4), :] = from_left[r // 2, ch, take, :]
            zs[0, ch * 4 + r, pl.ds(PAD + cells, 4), :] = from_right[r // 2, ch, take, :]

    @pl.when(me == 0)
    def _():
        for ch in range(4):
            zs[0, ch * 4, pl.ds(PAD - 4, 4), :] = tail_zero[ch, pl.ds(0, 4), :]
            total = tails_in[wrap_from, ch]
            for j in range(wrap_from + 1, n):
                total = total + tails_in[j, ch]
            for r in range(2, rows_dev):
                zs[0, ch * 4 + r, pl.ds(PAD - 4, 4), :] = total[(r % 2) * 4 : (r % 2) * 4 + 4]

    ends = []
    for r in range(rows_dev):
        room = lengths[r] - start
        end = jnp.clip(room, 0, cells)
        ends.append(end)
        over = jnp.clip(room - cells, 0, 5)
        short = jnp.clip(room, 0, 4)
        for ch in range(4):
            upper = zs[0, ch * 4 + r, pl.ds(PAD + end - 3, 8), :]
            lower = zs[0, ch * 4 + r, pl.ds(PAD - 4, 8), :]
            if r != 1:
                head_rows[r, ch, pl.ds(16, 4), :] = heads[r // 2, ch, pl.ds((r % 2) * 4, 4), :]
                upper = jnp.where(
                    index8 - 3 >= over, head_rows[r, ch, pl.ds(13 - over, 8), :], upper
                )
                lower = jnp.where(
                    index8 - 4 >= short, head_rows[r, ch, pl.ds(12 - short, 8), :], lower
                )
            zh[0, ch, pl.ds(PAD + r * 16, 8), :] = lower
            zh[0, ch, pl.ds(PAD + r * 16 + 8, 8), :] = upper

    for t in range(SUB):
        substep(
            zs, zh, products, weights, t % 2, (t + 1) % 2, cells, rows_dev, ends, t < SUB - 1
        )

    scale = GLON_DEV / (3.0 * cells)
    near = me * GLON_DEV - 1 + lax.broadcasted_iota(jnp.int32, (8, cells), 0)
    for r in range(rows_dev):
        body = pl.ds(PAD, cells)
        total = zs[0, r, body, :] + zs[0, 4 + r, body, :] + zs[0, 8 + r, body, :]
        delta = (total - start_sum[r]) * scale
        table = (own_ref[pl.ds(r, 1), :] == near).astype(F32)
        terms = jnp.dot(
            table, delta, precision=lax.Precision.HIGHEST, preferred_element_type=F32
        )
        c_left[pl.ds(r, 1), :] = terms[0:1]
        c_right[pl.ds(r, 1), :] = terms[GLON_DEV + 1 : GLON_DEV + 2]
        for g in range(GLON_DEV):
            co_ref[g, pl.ds(r, 1), :] = terms[g + 1 : g + 2]
    part_left = copy(c_left, c_from_right, sends.at[6], recvs.at[7], left, lat)
    part_right = copy(c_right, c_from_left, sends.at[7], recvs.at[8], right, lat)
    store_state(zo_ref, zs, cells, rows_dev)
    part_left.start()
    part_right.start()

    copy(m_first, m_halo.at[0], sends.at[2], recvs.at[2], south_lon, south_lat).wait()
    copy(m_last, m_halo.at[1], sends.at[3], recvs.at[3], north_lon, north_lat).wait()
    for r in range(rows_dev):
        take = (r % 2) * 4
        for ch in range(4):
            turned = ch if ch == 3 else 2 - ch
            sign = -1.0 if ch == 3 else 1.0
            base = PAD + r * 16
            for j in range(4):
                plain = m_halo[0, r // 2, ch, pl.ds(take + j, 1), :]
                pole = sign * m_halo[0, r // 2, turned, pl.ds(take + 3 - j, 1), :]
                mh[0, ch, pl.ds(base + j, 1), :] = jnp.where(at_south, pole, plain)
                plain = m_halo[1, r // 2, ch, pl.ds(take + j, 1), :]
                pole = sign * m_halo[1, r // 2, turned, pl.ds(take + 3 - j, 1), :]
                mh[0, ch, pl.ds(base + 11 + j, 1), :] = jnp.where(at_north, pole, plain)
            mh[0, ch, pl.ds(base + 4, 4), :] = ms[0, ch * 4 + r, pl.ds(PAD, 4), :]
            mh[0, ch, pl.ds(base + 8, 3), :] = ms[0, ch * 4 + r, pl.ds(PAD + cells - 3, 3), :]
            mh[0, ch, pl.ds(base + 15, 1), :] = jnp.zeros((1, 128), F32)
    for t in range(SUB):
        substep(
            ms, mh, products, weights, t % 2, (t + 1) % 2, cells, rows_dev, None, t < SUB - 1
        )
    store_state(mo_ref, ms, cells, rows_dev)
    part_left.wait()
    part_right.wait()
    for r in range(rows_dev):
        co_ref[0, pl.ds(r, 1), :] += c_from_left[pl.ds(r, 1), :]
        co_ref[GLON_DEV - 1, pl.ds(r, 1), :] += c_from_right[pl.ds(r, 1), :]


def solution(mesh):
    n, n_lat = mesh.shape["lon"], mesh.shape["lat"]

    def shards(
        zonal_state, zonal_courant, zonal_length, zonal_owner, merid_state, merid_courant, mixing
    ):
        nv, lev, wid, rows_dev, cells = zonal_state.shape
        flat = nv * lev * wid * rows_dev
        vmem = pl.BlockSpec(memory_space=pltpu.VMEM)
        state = pltpu.VMEM((2, 16, cells + 2 * PAD, 128), F32)
        strips = pltpu.VMEM((2, 4, 16 * rows_dev + 2 * PAD, 128), F32)
        packet = pltpu.VMEM((2, 4, 8, 128), F32)
        small = pltpu.VMEM((8, 128), F32)
        dma = pltpu.SemaphoreType.DMA
        zo, mo, co = pl.pallas_call(
            functools.partial(kernel, n, n_lat, cells, rows_dev),
            out_shape=(
                jax.ShapeDtypeStruct((flat, cells), F32),
                jax.ShapeDtypeStruct((flat, cells), F32),
                jax.ShapeDtypeStruct((GLON_DEV, rows_dev, nv * lev), F32),
            ),
            in_specs=[pl.BlockSpec(memory_space=pltpu.SMEM)] + [vmem] * 6,
            out_specs=(vmem, vmem, vmem),
            scratch_shapes=[
                state, state, strips, strips,
                pltpu.VMEM((rows_dev * 3 * cells + 3 * 16 * rows_dev, 128), F32),
                pltpu.VMEM((256, 256), jnp.bfloat16),
                pltpu.VMEM((rows_dev, cells, 128), F32),
                packet, packet, packet, packet, packet,
                packet, packet, packet,
                pltpu.VMEM((n, 4, 8, 128), F32),
                pltpu.VMEM((4, 8, 128), F32),
                pltpu.VMEM((2, 2, 4, 8, 128), F32),
                pltpu.VMEM((rows_dev, 4, 32, 128), F32),
                small, small, small, small,
                dma((8,)), dma((9,)), dma((1,)), dma((n,)), dma((n,)),
            ],
            compiler_params=pltpu.CompilerParams(
                collective_id=0, has_side_effects=True, vmem_limit_bytes=48 * 1024 * 1024
            ),
        )(
            zonal_length,
            zonal_state.reshape(flat, cells),
            zonal_courant.reshape(lev * rows_dev, cells),
            zonal_owner,
            merid_state.reshape(flat, cells),
            merid_courant.reshape(lev * rows_dev, cells),
            mixing.reshape(nv * lev, lev),
        )
        return zo.reshape(zonal_state.shape), mo.reshape(merid_state.shape), co

    return jax.shard_map(
        shards,
        mesh=mesh,
        in_specs=(
            P(None, None, None, "lat", "lon"),
            P(None, "lat", "lon"),
            P("lat"),
            P("lat", "lon"),
            P(None, None, None, "lon", "lat"),
            P(None, "lon", "lat"),
            P(),
        ),
        out_specs=(
            P(None, None, None, "lat", "lon"),
            P(None, None, None, "lon", "lat"),
            P("lon", "lat", None),
        ),
        check_vma=False,
    )
```

time: 468 us -> 28.2 us (0.06); the launches traced: 459 us -> 27.8 us
  blocking collectives: 234 us -> 0 us
  local copies, waits for them, and re-layouts: 106 us -> 7.81 us
  starting transfers between devices: 47.3 us -> 0 us
  other arithmetic: 38.5 us -> 0 us
  matrix products: 25.9 us -> 0 us
  Pallas kernels: 0 us -> 19.4 us
  waiting for transfers between devices: 6.03 us -> 0 us
    psum x4 -> x0, blocking collectives: 234 us -> none  [cycle_ends(): return lax.psum((head_part, tail_part), 'lon')]
    ppermute x22 -> x0, starting transfers between devices: 47.3 us -> none  [the longest x7 26.2 us: padded_2(): lax.ppermute(tail, axis, [(i, (i + 1) % count) for i in range(ends)])]
    slice x37 -> x0, local copies, waits for them, and re-layouts: 34.1 us -> none  [the longest x8 9.51 us: across_terms(): field_now[:, :, :2]]
    scatter x8 -> x0, local copies, waits for them, and re-layouts: 29.9 us -> none  [the longest x4 21.8 us: shards(): forward_side.at[..., -1]]
    dot_general x9 -> x0, matrix products: 25.9 us -> none  [the longest x8 25.6 us: tendency(): jnp.einsum('vkj,vjwrx->vkwrx', mixing, field_now, precision=lax.Precision...]
    pallas_call x0 -> x1, Pallas kernels: none -> 19.4 us  [shards(): pl.pallas_call(functools.partial(kernel, n, n_lat, cells, rows_dev), out_...]
    ppermute x10 -> x0, local copies, waits for them, and re-layouts: 18.3 us -> none  [the longest x5 9.15 us: padded_2(): lax.ppermute(tail, axis, [(i, (i + 1) % count) for i in range(ends)])]
    concatenate x5 -> x0, other arithmetic: 13.2 us -> none  [padded_2(): jnp.concatenate([lax.ppermute(tail, axis, [(i, (i + 1) % count) for i in...]
  transfers between devices with their start and end apart: 22 -> 0, of which waited for: 4 -> 0; matrix products, arithmetic and copies ran while one was open for 36% -> 0% of each run, Pallas kernels for 0% -> 0%
where the time goes in v1:
time: 28.2 us; the launch traced here: 27.8 us
  Pallas kernels  19.4 us (69%)
  local copies, waits for them, and re-layouts  7.81 us (28%)
  between operations  0.66 us (2%)
    pallas_call x1, Pallas kernels, shards(): pl.pallas_call(functools.partial(kernel, n, n_lat, cells, rows_dev), out_...  19.4 us
    unnamed x17, local copies, waits for them, and re-layouts  7.81 us

profile of v1, /device:TPU:0, one launch (start us, length us, event | category | flops | bytes accessed | tf_op | source)
XLA Modules:
  0.0 27.8 jit_solution(542141747069609919)
XLA Ops:
  0.6 0.0 copy-start.5
  0.6 0.0 copy-start.6
  0.7 0.7 %copy-done.5 = s32[4,128]{1,0:T(4,128)S(1)} copy-done((s32[4,128]{1,0:T(4,128)S(1)}, s32[4,128]{1,0:T(4,128)}, u32[]{:S(2)}) %copy-start.5) | copy-done | bytes 2072
  1.3 0.0 copy-done.6
  1.3 0.0 copy-start
  1.3 1.1 %copy-done = f32[4,32,3,4,128]{4,3,2,1,0:T(4,128)S(1)} copy-done((f32[4,32,3,4,128]{4,3,2,1,0:T(4,128)S(1)}, f32[4,32,3,4,128]{4,3,2,1,0:T(4,128)}, u32[]{:S(2)}) %copy-start) | copy-done | bytes 786456
  2.5 0.0 copy-start.1
  2.5 1.1 %copy-done.1 = f32[4,32,3,4,128]{4,3,2,1,0:T(4,128)S(1)} copy-done((f32[4,32,3,4,128]{4,3,2,1,0:T(4,128)S(1)}, f32[4,32,3,4,128]{4,3,2,1,0:T(4,128)}, u32[]{:S(2)}) %copy-start.1) | copy-done | bytes 786456
  3.6 0.0 copy-start.2
  3.6 0.8 %copy-done.2 = f32[32,4,128]{2,1,0:T(4,128)S(1)} copy-done((f32[32,4,128]{2,1,0:T(4,128)S(1)}, f32[32,4,128]{2,1,0:T(4,128)}, u32[]{:S(2)}) %copy-start.2) | copy-done | bytes 65560
  4.4 0.0 copy-start.3
  4.4 0.8 %copy-done.3 = f32[32,4,128]{2,1,0:T(4,128)S(1)} copy-done((f32[32,4,128]{2,1,0:T(4,128)S(1)}, f32[32,4,128]{2,1,0:T(4,128)}, u32[]{:S(2)}) %copy-start.3) | copy-done | bytes 65560
  5.3 0.0 copy-start.4
  5.3 0.8 %copy-done.4 = f32[4,32,32]{2,1,0:T(8,128)S(1)} copy-done((f32[4,32,32]{2,1,0:T(8,128)S(1)}, f32[4,32,32]{2,1,0:T(8,128)}, u32[]{:S(2)}) %copy-start.4) | copy-done | bytes 16408
  6.1 19.4 %shard_map.94 = (f32[1536,128]{1,0:T(8,128)S(1)}, f32[1536,128]{1,0:T(8,128)S(1)}, f32[4,4,128]{2,1,0:T(4,128)S(1)}) custom-call(s32[4]{0:T(128)S(1)} %copy-done.6, f32[1536,128]{1,0:T(8,128)S(1)} %bitcast.7, f32[128,128]{1,0:T(8,128)S(1)} %bitcast.11, s32[4,128]{1,0:T(4,128)S(1)} %copy-done.5, f32[1536,128]{1,0:T(8,128)S(1)} %bitcast.8, ...), custom_call_target="tpu_custom_call" | custom-call | tf_op jit(solution)/shard_map/pallas_call | solution.py:364
  25.5 0.9 %copy.13 = f32[4,32,3,4,128]{4,3,2,1,0:T(4,128)} copy(f32[4,32,3,4,128]{4,3,2,1,0:T(4,128)S(1)} %bitcast.10) | data formatting | bytes 1572864
  26.4 0.9 %copy.14 = f32[4,32,3,4,128]{4,3,2,1,0:T(4,128)} copy(f32[4,32,3,4,128]{4,3,2,1,0:T(4,128)S(1)} %bitcast.9) | data formatting | bytes 1572864
  27.2 0.6 %copy.15 = f32[4,4,128]{2,1,0:T(4,128)} copy(f32[4,4,128]{2,1,0:T(4,128)S(1)} %get-tuple-element.14) | data formatting | bytes 16384
Async XLA Ops:
  0.6 0.7 %copy-start.5 = (s32[4,128]{1,0:T(4,128)S(1)}, s32[4,128]{1,0:T(4,128)}, u32[]{:S(2)}) copy-start(s32[4,128]{1,0:T(4,128)} %own_ref.1) | copy-start | bytes 6148
  0.6 0.7 %copy-start.6 = (s32[4]{0:T(128)S(1)}, s32[4]{0:T(128)}, u32[]{:S(2)}) copy-start(s32[4]{0:T(128)} %len_ref.1) | copy-start | bytes 52
  1.3 1.1 %copy-start = (f32[4,32,3,4,128]{4,3,2,1,0:T(4,128)S(1)}, f32[4,32,3,4,128]{4,3,2,1,0:T(4,128)}, u32[]{:S(2)}) copy-start(f32[4,32,3,4,128]{4,3,2,1,0:T(4,128)} %param.7) | copy-start | bytes 2359300
  2.5 1.1 %copy-start.1 = (f32[4,32,3,4,128]{4,3,2,1,0:T(4,128)S(1)}, f32[4,32,3,4,128]{4,3,2,1,0:T(4,128)}, u32[]{:S(2)}) copy-start(f32[4,32,3,4,128]{4,3,2,1,0:T(4,128)} %param.11) | copy-start | bytes 2359300
  3.6 0.8 %copy-start.2 = (f32[32,4,128]{2,1,0:T(4,128)S(1)}, f32[32,4,128]{2,1,0:T(4,128)}, u32[]{:S(2)}) copy-start(f32[32,4,128]{2,1,0:T(4,128)} %param.8) | copy-start | bytes 196612
  4.4 0.8 %copy-start.3 = (f32[32,4,128]{2,1,0:T(4,128)S(1)}, f32[32,4,128]{2,1,0:T(4,128)}, u32[]{:S(2)}) copy-start(f32[32,4,128]{2,1,0:T(4,128)} %param.12) | copy-start | bytes 196612
  5.3 0.8 %copy-start.4 = (f32[4,32,32]{2,1,0:T(8,128)S(1)}, f32[4,32,32]{2,1,0:T(8,128)}, u32[]{:S(2)}) copy-start(f32[4,32,32]{2,1,0:T(8,128)} %param.13) | copy-start | bytes 49156

commit v2 on v1

v2 whole, which is shorter than its diff:
```python
import functools

import jax
import jax.numpy as jnp
from jax import lax
from jax.experimental import pallas as pl
from jax.experimental.pallas import tpu as pltpu
from jax.sharding import PartitionSpec as P

SUB = 4
GLON_DEV = 4
PAD = 8
MESH = pl.DeviceIdType.MESH
F32 = jnp.float32


def mix_into(products, at, fields, weights):
    wide = jnp.concatenate(fields, axis=0)
    high = wide.astype(jnp.bfloat16)
    low = (wide - high.astype(F32)).astype(jnp.bfloat16)
    out = jnp.dot(jnp.concatenate([high, low], axis=1), weights[...], preferred_element_type=F32)
    half = out.shape[1] // 2
    products[pl.ds(at, wide.shape[0]), :] = out[:, :half] + out[:, half:]


def updated(now, ahead, behind, courant, product):
    c_ahead = 0.3 - 0.5 * courant
    c_behind = 0.3 + 0.5 * courant
    x0, x1, x2 = now
    local = (0.3 * x0 + 0.1 * x1, 0.2 * x1 + 0.1 * (x0 + x2), 0.3 * x2 + 0.1 * x1)
    return [
        local[w] + c_ahead * ahead[w] + c_behind * behind[w] + product[w] for w in range(3)
    ]


def substep(state, strips, products, weights, src, dst, cells, rows_dev, tails, strips_too):
    rows = 3 * cells
    for r in range(rows_dev):
        mix_into(
            products,
            r * rows,
            [state[src][w * 4 + r, pl.ds(PAD, cells), :] for w in range(3)],
            weights,
        )
    srows = 16 * rows_dev
    if strips_too:
        mix_into(
            products,
            rows_dev * rows,
            [strips[src][w, pl.ds(PAD, srows), :] for w in range(3)],
            weights,
        )
    for r in range(rows_dev):
        for w in range(3):
            edge = PAD + r * 16 + 3
            state[src][w * 4 + r, pl.ds(PAD - 1, 1), :] = strips[src][w, pl.ds(edge, 1), :]
            state[src][w * 4 + r, pl.ds(PAD + cells, 1), :] = strips[src][w, pl.ds(edge + 8, 1), :]
    step = 32
    for r in range(rows_dev):
        for at in range(0, cells, step):
            now = [state[src][w * 4 + r, pl.ds(PAD + at, step), :] for w in range(3)]
            ahead = [state[src][w * 4 + r, pl.ds(PAD + at + 1, step), :] for w in range(3)]
            behind = [state[src][w * 4 + r, pl.ds(PAD + at - 1, step), :] for w in range(3)]
            courant = state[0][12 + r, pl.ds(PAD + at, step), :]
            product = [
                products[pl.ds(r * rows + w * cells + at, step), :] for w in range(3)
            ]
            if tails is not None:
                index = at + lax.broadcasted_iota(jnp.int32, (step, 128), 0)
                end = tails[r]
                for w in range(3):
                    beyond = strips[src][w, pl.ds(PAD + r * 16 + 11, 1), :]
                    ahead[w] = jnp.where(index == end - 1, beyond, ahead[w])
            new = updated(now, ahead, behind, courant, product)
            for w in range(3):
                value = new[w]
                if tails is not None:
                    value = jnp.where(index < end, value, now[w])
                state[dst][w * 4 + r, pl.ds(PAD + at, step), :] = value
    if strips_too:
        base = rows_dev * rows
        for at in range(0, srows, step):
            now = [strips[src][w, pl.ds(PAD + at, step), :] for w in range(3)]
            ahead = [strips[src][w, pl.ds(PAD + at + 1, step), :] for w in range(3)]
            behind = [strips[src][w, pl.ds(PAD + at - 1, step), :] for w in range(3)]
            courant = strips[0][3, pl.ds(PAD + at, step), :]
            product = [products[pl.ds(base + w * srows + at, step), :] for w in range(3)]
            new = updated(now, ahead, behind, courant, product)
            for w in range(3):
                strips[dst][w, pl.ds(PAD + at, step), :] = new[w]


def load_state(state, field, courant, cells, rows_dev):
    for r in range(rows_dev):
        for w in range(3):
            at = w * rows_dev + r
            block = field[pl.ds(at, 128, stride=3 * rows_dev), :]
            state[w * 4 + r, pl.ds(PAD, cells), :] = block.T
        levels = courant[pl.ds(r, 32, stride=rows_dev), :]
        state[12 + r, pl.ds(PAD, cells), :] = jnp.concatenate([levels] * 4, axis=0).T


def store_state(out, state, cells, rows_dev):
    for r in range(rows_dev):
        for w in range(3):
            at = w * rows_dev + r
            out[pl.ds(at, 128, stride=3 * rows_dev), :] = state[w * 4 + r, pl.ds(PAD, cells), :].T


def pack_ends(first, last, state, cells, rows_dev):
    for r in range(rows_dev):
        for ch in range(4):
            put = pl.ds((r % 2) * 4, 4)
            first[r // 2, ch, put, :] = state[ch * 4 + r, pl.ds(PAD, 4), :]
            last[r // 2, ch, put, :] = state[ch * 4 + r, pl.ds(PAD + cells - 4, 4), :]


def kernel(
    n, n_lat, cells, rows_dev,
    len_hbm, z_hbm, zc_hbm, own_hbm, m_hbm, mc_hbm, mix_hbm,
    zs, ms, ms1, mh, mh1, weights, co_ref,
    len_ref, z_ref, zc_ref, own_ref, m_ref, mc_ref, mix_ref, in_sems,
    zs1, zh, zh1, products, start_sum,
    z_first, z_last, z_tail, m_first, m_last,
    from_left, from_right, heads, tails_in, tail_zero, m_halo, head_rows,
    c_left, c_right, c_from_left, c_from_right,
    sends, recvs, tail_sends, tail_recvs, head_sends,
):
    me = lax.axis_index("lon")
    lat = lax.axis_index("lat")
    right, left = lax.rem(me + 1, n), lax.rem(me + n - 1, n)
    partner = lax.rem(me + n // 2, n)
    wrap_from = n // 4 - 1
    mid = n // 2
    start = me * cells
    loads = [
        pltpu.make_async_copy(src, dst, in_sems.at[i])
        for i, (src, dst) in enumerate(
            (
                (z_hbm, z_ref), (zc_hbm, zc_ref), (len_hbm, len_ref), (m_hbm, m_ref),
                (mc_hbm, mc_ref), (mix_hbm, mix_ref), (own_hbm, own_ref),
            )
        )
    ]
    for load in loads:
        load.start()
    barrier = pltpu.get_barrier_semaphore()

    def greet(lon_to, lat_to):
        pl.semaphore_signal(barrier, inc=1, device_id=(lon_to, lat_to), device_id_type=MESH)

    greet(left, lat)
    greet(right, lat)
    at_south, at_north = lat == 0, lat == n_lat - 1
    south_lon = jnp.where(at_south, partner, me)
    south_lat = jnp.where(at_south, 0, lat - 1)
    north_lon = jnp.where(at_north, partner, me)
    north_lat = jnp.where(at_north, n_lat - 1, lat + 1)
    greet(south_lon, south_lat)
    greet(north_lon, north_lat)

    @pl.when(me == 0)
    def _():
        for j in range(wrap_from, n):
            greet(j, lat)

    @pl.when(me >= wrap_from)
    def _():
        greet(0, lat)

    for load in loads[:3]:
        load.wait()
    load_state(zs, z_ref, zc_ref, cells, rows_dev)
    pack_ends(z_first, z_last, zs, cells, rows_dev)
    lengths = [len_ref[r] for r in range(rows_dev)]
    index8 = lax.broadcasted_iota(jnp.int32, (8, 128), 0)
    for r in range(rows_dev):
        at = jnp.clip(lengths[r] - 4 - start, -4, cells)
        cell = lengths[r] - 4 - start + index8
        own = (cell >= 0) & (cell < cells)
        for ch in range(4):
            value = zs[ch * 4 + r, pl.ds(PAD + at, 8), :]
            z_tail[r // 2, ch, pl.ds((r % 2) * 4, 4), :] = jnp.where(own, value, 0.0)[:4]
    extra = jnp.where(me == 0, n - wrap_from, jnp.where(me >= wrap_from, 1, 0))
    pl.semaphore_wait(barrier, 4 + extra)

    def copy(src, dst, send, recv, lon_to, lat_to):
        return pltpu.make_async_remote_copy(
            src_ref=src, dst_ref=dst, send_sem=send, recv_sem=recv,
            device_id=(lon_to, lat_to), device_id_type=MESH,
        )

    def head_copy(j):
        return copy(z_first.at[1], heads.at[1], head_sends.at[j], recvs.at[4], j, lat)

    head_mid = copy(z_first.at[0], heads.at[0], sends.at[5], recvs.at[5], mid, lat)
    tail_mid = copy(z_tail.at[0], tail_zero, sends.at[5], recvs.at[6], 0, lat)

    def tail_copy(j):
        return copy(z_tail.at[1], tails_in.at[j], sends.at[4], tail_recvs.at[j], 0, lat)

    @pl.when(me == 0)
    def _():
        for j in range(wrap_from, n):
            head_copy(j).start()
        head_mid.start()

    @pl.when(me >= wrap_from)
    def _():
        tail_copy(me).start()

    @pl.when(me == mid)
    def _():
        tail_mid.start()

    to_right = copy(z_last, from_left, sends.at[0], recvs.at[0], right, lat)
    to_left = copy(z_first, from_right, sends.at[1], recvs.at[1], left, lat)
    to_right.start()
    to_left.start()
    for load in loads[3:]:
        load.wait()
    load_state(ms, m_ref, mc_ref, cells, rows_dev)
    pack_ends(m_first, m_last, ms, cells, rows_dev)
    south_slot = jnp.where(at_south, 0, 1)
    north_slot = jnp.where(at_north, 1, 0)
    to_south = copy(
        m_first, m_halo.at[south_slot], sends.at[2], recvs.at[2 + south_slot], south_lon, south_lat
    )
    to_north = copy(
        m_last, m_halo.at[north_slot], sends.at[3], recvs.at[2 + north_slot], north_lon, north_lat
    )
    to_south.start()
    to_north.start()

    tiled = jnp.concatenate([mix_ref[...]] * 4, axis=1)
    block_of = lambda axis: lax.broadcasted_iota(jnp.int32, (128, 128), axis) // 32
    matrix = jnp.where(block_of(0) == block_of(1), tiled, 0.0).T
    w_high = matrix.astype(jnp.bfloat16)
    w_low = (matrix - w_high.astype(F32)).astype(jnp.bfloat16)
    pair = jnp.concatenate([w_high, w_low], axis=1)
    weights[pl.ds(0, 128), :] = pair
    weights[pl.ds(128, 128), :] = pair
    for r in range(rows_dev):
        body = pl.ds(PAD, cells)
        start_sum[r] = zs[r, body, :] + zs[4 + r, body, :] + zs[8 + r, body, :]
    for buf in (zh, zh1, mh, mh1):
        for ch in range(3):
            buf[ch, pl.ds(0, 8), :] = jnp.zeros((8, 128), F32)
            buf[ch, pl.ds(PAD + 16 * rows_dev, 8), :] = jnp.zeros((8, 128), F32)

    copy(m_first, m_halo.at[0], sends.at[2], recvs.at[2], south_lon, south_lat).wait()
    copy(m_last, m_halo.at[1], sends.at[3], recvs.at[3], north_lon, north_lat).wait()
    for r in range(rows_dev):
        take = (r % 2) * 4
        for ch in range(4):
            turned = ch if ch == 3 else 2 - ch
            sign = -1.0 if ch == 3 else 1.0
            base = PAD + r * 16
            for j in range(4):
                plain = m_halo[0, r // 2, ch, pl.ds(take + j, 1), :]
                pole = sign * m_halo[0, r // 2, turned, pl.ds(take + 3 - j, 1), :]
                mh[ch, pl.ds(base + j, 1), :] = jnp.where(at_south, pole, plain)
                plain = m_halo[1, r // 2, ch, pl.ds(take + j, 1), :]
                pole = sign * m_halo[1, r // 2, turned, pl.ds(take + 3 - j, 1), :]
                mh[ch, pl.ds(base + 11 + j, 1), :] = jnp.where(at_north, pole, plain)
            mh[ch, pl.ds(base + 4, 4), :] = ms[ch * 4 + r, pl.ds(PAD, 4), :]
            mh[ch, pl.ds(base + 8, 3), :] = ms[ch * 4 + r, pl.ds(PAD + cells - 3, 3), :]
            mh[ch, pl.ds(base + 15, 1), :] = jnp.zeros((1, 128), F32)
    for t in range(SUB // 2):
        substep(
            (ms, ms1), (mh, mh1), products, weights, t % 2, (t + 1) % 2, cells, rows_dev, None,
            True,
        )
    to_right.wait()
    to_left.wait()

    @pl.when(me >= wrap_from)
    def _():
        tail_copy(me).wait_send()
        head_copy(me).wait_recv()

    @pl.when(me == mid)
    def _():
        tail_mid.wait_send()
        head_mid.wait_recv()

    @pl.when(me == 0)
    def _():
        for j in range(wrap_from, n):
            head_copy(j).wait_send()
            tail_copy(j).wait_recv()
        head_mid.wait_send()
        tail_mid.wait_recv()

    for r in range(rows_dev):
        take = pl.ds((r % 2) * 4, 4)
        for ch in range(4):
            zs[ch * 4 + r, pl.ds(PAD - 4, 4), :] = from_left[r // 2, ch, take, :]
            zs[ch * 4 + r, pl.ds(PAD + cells, 4), :] = from_right[r // 2, ch, take, :]

    @pl.when(me == 0)
    def _():
        for ch in range(4):
            zs[ch * 4, pl.ds(PAD - 4, 4), :] = tail_zero[ch, pl.ds(0, 4), :]
            total = tails_in[wrap_from, ch]
            for j in range(wrap_from + 1, n):
                total = total + tails_in[j, ch]
            for r in range(2, rows_dev):
                zs[ch * 4 + r, pl.ds(PAD - 4, 4), :] = total[(r % 2) * 4 : (r % 2) * 4 + 4]

    ends = []
    for r in range(rows_dev):
        room = lengths[r] - start
        end = jnp.clip(room, 0, cells)
        ends.append(end)
        over = jnp.clip(room - cells, 0, 5)
        short = jnp.clip(room, 0, 4)
        for ch in range(4):
            upper = zs[ch * 4 + r, pl.ds(PAD + end - 3, 8), :]
            lower = zs[ch * 4 + r, pl.ds(PAD - 4, 8), :]
            if r != 1:
                head_rows[r, ch, pl.ds(16, 4), :] = heads[r // 2, ch, pl.ds((r % 2) * 4, 4), :]
                upper = jnp.where(
                    index8 - 3 >= over, head_rows[r, ch, pl.ds(13 - over, 8), :], upper
                )
                lower = jnp.where(
                    index8 - 4 >= short, head_rows[r, ch, pl.ds(12 - short, 8), :], lower
                )
            zh[ch, pl.ds(PAD + r * 16, 8), :] = lower
            zh[ch, pl.ds(PAD + r * 16 + 8, 8), :] = upper

    for t in range(SUB):
        substep(
            (zs, zs1), (zh, zh1), products, weights, t % 2, (t + 1) % 2, cells, rows_dev, ends,
            t < SUB - 1,
        )

    scale = GLON_DEV / (3.0 * cells)
    near = me * GLON_DEV - 1 + lax.broadcasted_iota(jnp.int32, (8, cells), 0)
    for r in range(rows_dev):
        body = pl.ds(PAD, cells)
        total = zs[r, body, :] + zs[4 + r, body, :] + zs[8 + r, body, :]
        delta = (total - start_sum[r]) * scale
        table = (own_ref[pl.ds(r, 1), :] == near).astype(F32)
        terms = jnp.dot(
            table, delta, precision=lax.Precision.HIGHEST, preferred_element_type=F32
        )
        c_left[pl.ds(r, 1), :] = terms[0:1]
        c_right[pl.ds(r, 1), :] = terms[GLON_DEV + 1 : GLON_DEV + 2]
        for g in range(GLON_DEV):
            co_ref[g, pl.ds(r, 1), :] = terms[g + 1 : g + 2]
    part_left = copy(c_left, c_from_right, sends.at[6], recvs.at[7], left, lat)
    part_right = copy(c_right, c_from_left, sends.at[7], recvs.at[8], right, lat)
    part_left.start()
    part_right.start()

    for t in range(SUB // 2, SUB - 1):
        substep(
            (ms, ms1), (mh, mh1), products, weights, t % 2, (t + 1) % 2, cells, rows_dev, None,
            True,
        )
    part_left.wait()
    part_right.wait()
    for r in range(rows_dev):
        co_ref[0, pl.ds(r, 1), :] += c_from_left[pl.ds(r, 1), :]
        co_ref[GLON_DEV - 1, pl.ds(r, 1), :] += c_from_right[pl.ds(r, 1), :]


def finish(
    cells, rows_dev,
    zs, ms, ms1, mh, mh1, weights, co_in,
    zo_hbm, mo_hbm, co_hbm,
    zo, mo, products, sems,
):
    co_copy = pltpu.make_async_copy(co_in, co_hbm, sems.at[2])
    co_copy.start()
    store_state(zo, zs, cells, rows_dev)
    zo_copy = pltpu.make_async_copy(zo, zo_hbm, sems.at[0])
    zo_copy.start()
    substep(
        (ms, ms1), (mh, mh1), products, weights, (SUB - 1) % 2, SUB % 2, cells, rows_dev, None, False
    )
    store_state(mo, ms, cells, rows_dev)
    mo_copy = pltpu.make_async_copy(mo, mo_hbm, sems.at[1])
    mo_copy.start()
    co_copy.wait()
    zo_copy.wait()
    mo_copy.wait()


def solution(mesh):
    n, n_lat = mesh.shape["lon"], mesh.shape["lat"]

    def shards(
        zonal_state, zonal_courant, zonal_length, zonal_owner, merid_state, merid_courant, mixing
    ):
        nv, lev, wid, rows_dev, cells = zonal_state.shape
        flat = nv * lev * wid * rows_dev
        vmem = pl.BlockSpec(memory_space=pltpu.VMEM)
        hbm = pl.BlockSpec(memory_space=pltpu.HBM)
        shape = jax.ShapeDtypeStruct
        state = (16, cells + 2 * PAD, 128)
        strips = (4, 16 * rows_dev + 2 * PAD, 128)
        packet = pltpu.VMEM((2, 4, 8, 128), F32)
        small = pltpu.VMEM((8, 128), F32)
        products = pltpu.VMEM((rows_dev * 3 * cells + 3 * 16 * rows_dev, 128), F32)
        dma = pltpu.SemaphoreType.DMA
        held = pl.pallas_call(
            functools.partial(kernel, n, n_lat, cells, rows_dev),
            out_shape=(
                shape(state, F32), shape(state, F32), shape(state, F32),
                shape(strips, F32), shape(strips, F32),
                shape((256, 256), jnp.bfloat16),
                shape((GLON_DEV, rows_dev, nv * lev), F32),
            ),
            in_specs=[hbm] * 7,
            out_specs=(vmem,) * 7,
            scratch_shapes=[
                pltpu.SMEM((rows_dev,), jnp.int32),
                pltpu.VMEM((flat, cells), F32),
                pltpu.VMEM((lev * rows_dev, cells), F32),
                pltpu.VMEM((rows_dev, cells), jnp.int32),
                pltpu.VMEM((flat, cells), F32),
                pltpu.VMEM((lev * rows_dev, cells), F32),
                pltpu.VMEM((nv * lev, lev), F32),
                dma((7,)),
                pltpu.VMEM(state, F32), pltpu.VMEM(strips, F32), pltpu.VMEM(strips, F32),
                products,
                pltpu.VMEM((rows_dev, cells, 128), F32),
                packet, packet, packet, packet, packet,
                packet, packet, packet,
                pltpu.VMEM((n, 4, 8, 128), F32),
                pltpu.VMEM((4, 8, 128), F32),
                pltpu.VMEM((2, 2, 4, 8, 128), F32),
                pltpu.VMEM((rows_dev, 4, 32, 128), F32),
                small, small, small, small,
                dma((8,)), dma((9,)), dma((1,)), dma((n,)), dma((n,)),
            ],
            compiler_params=pltpu.CompilerParams(
                collective_id=0, has_side_effects=True, vmem_limit_bytes=48 * 1024 * 1024
            ),
        )(
            *(
                pltpu.with_memory_space_constraint(value, pltpu.HBM)
                for value in (
                    zonal_length,
                    zonal_state.reshape(flat, cells),
                    zonal_courant.reshape(lev * rows_dev, cells),
                    zonal_owner,
                    merid_state.reshape(flat, cells),
                    merid_courant.reshape(lev * rows_dev, cells),
                    mixing.reshape(nv * lev, lev),
                )
            )
        )
        zo, mo, co = pl.pallas_call(
            functools.partial(finish, cells, rows_dev),
            out_shape=(
                shape((flat, cells), F32), shape((flat, cells), F32),
                shape((GLON_DEV, rows_dev, nv * lev), F32),
            ),
            in_specs=[vmem] * 7,
            out_specs=(hbm,) * 3,
            scratch_shapes=[
                pltpu.VMEM((flat, cells), F32), pltpu.VMEM((flat, cells), F32), products, dma((3,)),
            ],
            compiler_params=pltpu.CompilerParams(vmem_limit_bytes=40 * 1024 * 1024),
        )(*held)
        return zo.reshape(zonal_state.shape), mo.reshape(merid_state.shape), co

    return jax.shard_map(
        shards,
        mesh=mesh,
        in_specs=(
            P(None, None, None, "lat", "lon"),
            P(None, "lat", "lon"),
            P("lat"),
            P("lat", "lon"),
            P(None, None, None, "lon", "lat"),
            P(None, "lon", "lat"),
            P(),
        ),
        out_specs=(
            P(None, None, None, "lat", "lon"),
            P(None, None, None, "lon", "lat"),
            P("lon", "lat", None),
        ),
        check_vma=False,
    )
```

time: 28.2 us -> 21.2 us (0.75)
  local copies, waits for them, and re-layouts: 7.81 us -> 0 us
  Pallas kernels: 19.4 us -> 20.4 us
    unnamed x17 -> x0, local copies, waits for them, and re-layouts: 7.81 us -> none
    pallas_call x0 -> x1, Pallas kernels: none -> 1.53 us  [shards(): pl.pallas_call(functools.partial(finish, cells, rows_dev), out_shape=(sha...]
    pallas_call x1, Pallas kernels: 19.4 us -> 18.9 us  [shards(): pl.pallas_call(functools.partial(kernel, n, n_lat, cells, rows_dev), out_...]
where the time goes in v2:
time: 21.2 us; the launch traced here: 21 us
  Pallas kernels  20.4 us (96%)
  between operations  0.64 us (3%)
    pallas_call x1, Pallas kernels, shards(): pl.pallas_call(functools.partial(kernel, n, n_lat, cells, rows_dev), out_...  18.9 us
    pallas_call x1, Pallas kernels, shards(): pl.pallas_call(functools.partial(finish, cells, rows_dev), out_shape=(sha...  1.53 us

profile of v2, /device:TPU:0, one launch (start us, length us, event | category | flops | bytes accessed | tf_op | source)
XLA Modules:
  0.0 21.0 jit_solution(3262982326814328497)
XLA Ops:
  0.6 18.9 %shard_map.94 = (f32[16,144,128]{2,1,0:T(8,128)S(1)}, f32[16,144,128]{2,1,0:T(8,128)S(1)}, f32[16,144,128]{2,1,0:T(8,128)S(1)}, f32[4,80,128]{2,1,0:T(8,128)S(1)...) custom-call(s32[4]{0:T(128)} %len_hbm.1, f32[1536,128]{1,0:T(8,128)} %bitcast.7, ...), custom_call_target="tpu_custom_call" | custom-call | tf_op jit(solution)/shard_map/pallas_call | solution.py:408
  19.5 1.5 %shard_map.95 = (f32[1536,128]{1,0:T(8,128)}, f32[1536,128]{1,0:T(8,128)}, f32[4,4,128]{2,1,0:T(4,128)}) custom-call(f32[16,144,128]{2,1,0:T(8,128)S(1)} %get-tuple-element.13.zs, f32[16,144,128]{2,1,0:T(8,128)S(1)} %get-tuple-element.14.ms, f32[16,144,128]{2,1,0:T(8,128)S(1)} %get-tuple-element.15.ms1, f32[4,80,128]{2,1,0:T(8,128)S(1)} %get-tuple-element.16.mh, ...), custom_call_target="tpu_custom_call" | custom-call | tf_op jit(solution)/shard_map/pallas_call | solution.py:456

commit v3 on v2

--- a/solution.py
+++ b/solution.py
@@ -33,61 +33,49 @@
     ]
 
 
-def substep(state, strips, products, weights, src, dst, cells, rows_dev, tails, strips_too):
+def advance(src, dst, courants, products, weights, cells, rows_dev, ends):
     rows = 3 * cells
+    step = 32
     for r in range(rows_dev):
         mix_into(
             products,
             r * rows,
-            [state[src][w * 4 + r, pl.ds(PAD, cells), :] for w in range(3)],
+            [src[w * 4 + r, pl.ds(PAD, cells), :] for w in range(3)],
             weights,
         )
-    srows = 16 * rows_dev
-    if strips_too:
-        mix_into(
-            products,
-            rows_dev * rows,
-            [strips[src][w, pl.ds(PAD, srows), :] for w in range(3)],
-            weights,
-        )
-    for r in range(rows_dev):
-        for w in range(3):
-            edge = PAD + r * 16 + 3
-            state[src][w * 4 + r, pl.ds(PAD - 1, 1), :] = strips[src][w, pl.ds(edge, 1), :]
-            state[src][w * 4 + r, pl.ds(PAD + cells, 1), :] = strips[src][w, pl.ds(edge + 8, 1), :]
-    step = 32
     for r in range(rows_dev):
         for at in range(0, cells, step):
-            now = [state[src][w * 4 + r, pl.ds(PAD + at, step), :] for w in range(3)]
-            ahead = [state[src][w * 4 + r, pl.ds(PAD + at + 1, step), :] for w in range(3)]
-            behind = [state[src][w * 4 + r, pl.ds(PAD + at - 1, step), :] for w in range(3)]
-            courant = state[0][12 + r, pl.ds(PAD + at, step), :]
+            now = [src[w * 4 + r, pl.ds(PAD + at, step), :] for w in range(3)]
+            ahead = [src[w * 4 + r, pl.ds(PAD + at + 1, step), :] for w in range(3)]
+            behind = [src[w * 4 + r, pl.ds(PAD + at - 1, step), :] for w in range(3)]
+            courant = courants[12 + r, pl.ds(PAD + at, step), :]
             product = [
                 products[pl.ds(r * rows + w * cells + at, step), :] for w in range(3)
             ]
-            if tails is not None:
-                index = at + lax.broadcasted_iota(jnp.int32, (step, 128), 0)
-                end = tails[r]
-                for w in range(3):
-                    beyond = strips[src][w, pl.ds(PAD + r * 16 + 11, 1), :]
-                    ahead[w] = jnp.where(index == end - 1, beyond, ahead[w])
             new = updated(now, ahead, behind, courant, product)
             for w in range(3):
                 value = new[w]
-                if tails is not None:
-                    value = jnp.where(index < end, value, now[w])
-                state[dst][w * 4 + r, pl.ds(PAD + at, step), :] = value
-    if strips_too:
-        base = rows_dev * rows
-        for at in range(0, srows, step):
-            now = [strips[src][w, pl.ds(PAD + at, step), :] for w in range(3)]
-            ahead = [strips[src][w, pl.ds(PAD + at + 1, step), :] for w in range(3)]
-            behind = [strips[src][w, pl.ds(PAD + at - 1, step), :] for w in range(3)]
-            courant = strips[0][3, pl.ds(PAD + at, step), :]
-            product = [products[pl.ds(base + w * srows + at, step), :] for w in range(3)]
+                if ends is not None:
+                    index = at + lax.broadcasted_iota(jnp.int32, (step, 128), 0)
+                    value = jnp.where(index < ends[r], value, now[w])
+                dst[w * 4 + r, pl.ds(PAD + at, step), :] = value
+
+
+def advance_strips(first, second, products, weights, rows_dev):
+    rows = 32 * rows_dev
+    step = 32
+    for t in range(SUB):
+        src, dst = (first, second) if t % 2 == 0 else (second, first)
+        mix_into(products, 0, [src[w, pl.ds(PAD, rows), :] for w in range(3)], weights)
+        for at in range(0, rows, step):
+            now = [src[w, pl.ds(PAD + at, step), :] for w in range(3)]
+            ahead = [src[w, pl.ds(PAD + at + 1, step), :] for w in range(3)]
+            behind = [src[w, pl.ds(PAD + at - 1, step), :] for w in range(3)]
+            courant = first[3, pl.ds(PAD + at, step), :]
+            product = [products[pl.ds(w * rows + at, step), :] for w in range(3)]
             new = updated(now, ahead, behind, courant, product)
             for w in range(3):
-                strips[dst][w, pl.ds(PAD + at, step), :] = new[w]
+                dst[w, pl.ds(PAD + at, step), :] = new[w]
 
 
 def load_state(state, field, courant, cells, rows_dev):
@@ -118,9 +106,9 @@
 def kernel(
     n, n_lat, cells, rows_dev,
     len_hbm, z_hbm, zc_hbm, own_hbm, m_hbm, mc_hbm, mix_hbm,
-    zs, ms, ms1, mh, mh1, weights, co_ref,
+    zs2, ms, ms1, mh, weights, co_ref,
     len_ref, z_ref, zc_ref, own_ref, m_ref, mc_ref, mix_ref, in_sems,
-    zs1, zh, zh1, products, start_sum,
+    zs, zs1, ms2, mh1, zh, zh1, products,
     z_first, z_last, z_tail, m_first, m_last,
     from_left, from_right, heads, tails_in, tail_zero, m_halo, head_rows,
     c_left, c_right, c_from_left, c_from_right,
@@ -240,37 +228,17 @@
     pair = jnp.concatenate([w_high, w_low], axis=1)
     weights[pl.ds(0, 128), :] = pair
     weights[pl.ds(128, 128), :] = pair
-    for r in range(rows_dev):
-        body = pl.ds(PAD, cells)
-        start_sum[r] = zs[r, body, :] + zs[4 + r, body, :] + zs[8 + r, body, :]
     for buf in (zh, zh1, mh, mh1):
         for ch in range(3):
             buf[ch, pl.ds(0, 8), :] = jnp.zeros((8, 128), F32)
-            buf[ch, pl.ds(PAD + 16 * rows_dev, 8), :] = jnp.zeros((8, 128), F32)
-
-    copy(m_first, m_halo.at[0], sends.at[2], recvs.at[2], south_lon, south_lat).wait()
-    copy(m_last, m_halo.at[1], sends.at[3], recvs.at[3], north_lon, north_lat).wait()
-    for r in range(rows_dev):
-        take = (r % 2) * 4
-        for ch in range(4):
-            turned = ch if ch == 3 else 2 - ch
-            sign = -1.0 if ch == 3 else 1.0
-            base = PAD + r * 16
-            for j in range(4):
-                plain = m_halo[0, r // 2, ch, pl.ds(take + j, 1), :]
-                pole = sign * m_halo[0, r // 2, turned, pl.ds(take + 3 - j, 1), :]
-                mh[ch, pl.ds(base + j, 1), :] = jnp.where(at_south, pole, plain)
-                plain = m_halo[1, r // 2, ch, pl.ds(take + j, 1), :]
-                pole = sign * m_halo[1, r // 2, turned, pl.ds(take + 3 - j, 1), :]
-                mh[ch, pl.ds(base + 11 + j, 1), :] = jnp.where(at_north, pole, plain)
-            mh[ch, pl.ds(base + 4, 4), :] = ms[ch * 4 + r, pl.ds(PAD, 4), :]
-            mh[ch, pl.ds(base + 8, 3), :] = ms[ch * 4 + r, pl.ds(PAD + cells - 3, 3), :]
-            mh[ch, pl.ds(base + 15, 1), :] = jnp.zeros((1, 128), F32)
-    for t in range(SUB // 2):
-        substep(
-            (ms, ms1), (mh, mh1), products, weights, t % 2, (t + 1) % 2, cells, rows_dev, None,
-            True,
-        )
+            buf[ch, pl.ds(PAD + 32 * rows_dev, 8), :] = jnp.zeros((8, 128), F32)
+
+    ends = [jnp.clip(lengths[r] - start, 0, cells) for r in range(rows_dev)]
+    for src, dst in ((zs, zs1), (zs1, zs2), (zs2, zs1), (zs1, zs2)):
+        advance(src, dst, zs, products, weights, cells, rows_dev, ends)
+    for src, dst in ((ms, ms1), (ms1, ms2)):
+        advance(src, dst, ms, products, weights, cells, rows_dev, None)
+
     to_right.wait()
     to_left.wait()
 
@@ -308,39 +276,53 @@
             for r in range(2, rows_dev):
                 zs[ch * 4 + r, pl.ds(PAD - 4, 4), :] = total[(r % 2) * 4 : (r % 2) * 4 + 4]
 
-    ends = []
+    index16 = lax.broadcasted_iota(jnp.int32, (16, 128), 0)
     for r in range(rows_dev):
         room = lengths[r] - start
-        end = jnp.clip(room, 0, cells)
-        ends.append(end)
+        end = ends[r]
         over = jnp.clip(room - cells, 0, 5)
-        short = jnp.clip(room, 0, 4)
-        for ch in range(4):
-            upper = zs[ch * 4 + r, pl.ds(PAD + end - 3, 8), :]
-            lower = zs[ch * 4 + r, pl.ds(PAD - 4, 8), :]
+        short = jnp.clip(room, 0, 12)
+        for ch in range(4):
+            upper = zs[ch * 4 + r, pl.ds(PAD + end - 8, 16), :]
+            lower = zs[ch * 4 + r, pl.ds(PAD - 4, 16), :]
             if r != 1:
                 head_rows[r, ch, pl.ds(16, 4), :] = heads[r // 2, ch, pl.ds((r % 2) * 4, 4), :]
                 upper = jnp.where(
-                    index8 - 3 >= over, head_rows[r, ch, pl.ds(13 - over, 8), :], upper
+                    index16 - 8 >= over, head_rows[r, ch, pl.ds(8 - over, 16), :], upper
                 )
                 lower = jnp.where(
-                    index8 - 4 >= short, head_rows[r, ch, pl.ds(12 - short, 8), :], lower
+                    index16 - 4 >= short, head_rows[r, ch, pl.ds(12 - short, 16), :], lower
                 )
-            zh[ch, pl.ds(PAD + r * 16, 8), :] = lower
-            zh[ch, pl.ds(PAD + r * 16 + 8, 8), :] = upper
-
-    for t in range(SUB):
-        substep(
-            (zs, zs1), (zh, zh1), products, weights, t % 2, (t + 1) % 2, cells, rows_dev, ends,
-            t < SUB - 1,
-        )
+            zh[ch, pl.ds(PAD + r * 32, 16), :] = lower
+            zh[ch, pl.ds(PAD + r * 32 + 16, 16), :] = upper
+    advance_strips(zh, zh1, products, weights, rows_dev)
+    index4 = lax.broadcasted_iota(jnp.int32, (4, 128), 0)
+    for r in range(rows_dev):
+        base = PAD + r * 32
+        for w in range(3):
+            at = w * 4 + r
+            low = zs2[at, pl.ds(PAD, 4), :]
+            zs2[at, pl.ds(PAD, 4), :] = jnp.where(
+                index4 < ends[r], zh[w, pl.ds(base + 4, 4), :], low
+            )
+        for block in range(0, cells, 8):
+            ahead = block - ends[r]
+            inside = (index8 + ahead >= -4) & (index8 + ahead < 0)
+            take = base + 16 + jnp.clip(ahead + 8, -8, 8)
+            for w in range(3):
+                at = w * 4 + r
+                high = zs2[at, pl.ds(PAD + block, 8), :]
+                zs2[at, pl.ds(PAD + block, 8), :] = jnp.where(
+                    inside, zh[w, pl.ds(take, 8), :], high
+                )
 
     scale = GLON_DEV / (3.0 * cells)
     near = me * GLON_DEV - 1 + lax.broadcasted_iota(jnp.int32, (8, cells), 0)
     for r in range(rows_dev):
         body = pl.ds(PAD, cells)
-        total = zs[r, body, :] + zs[4 + r, body, :] + zs[8 + r, body, :]
-        delta = (total - start_sum[r]) * scale
+        before = zs[r, body, :] + zs[4 + r, body, :] + zs[8 + r, body, :]
+        after = zs2[r, body, :] + zs2[4 + r, body, :] + zs2[8 + r, body, :]
+        delta = (after - before) * scale
         table = (own_ref[pl.ds(r, 1), :] == near).astype(F32)
         terms = jnp.dot(
             table, delta, precision=lax.Precision.HIGHEST, preferred_element_type=F32
@@ -354,11 +336,27 @@
     part_left.start()
     part_right.start()
 
-    for t in range(SUB // 2, SUB - 1):
-        substep(
-            (ms, ms1), (mh, mh1), products, weights, t % 2, (t + 1) % 2, cells, rows_dev, None,
-            True,
-        )
+
+    copy(m_first, m_halo.at[0], sends.at[2], recvs.at[2], south_lon, south_lat).wait()
+    copy(m_last, m_halo.at[1], sends.at[3], recvs.at[3], north_lon, north_lat).wait()
+    for r in range(rows_dev):
+        take = (r % 2) * 4
+        for ch in range(4):
+            turned = ch if ch == 3 else 2 - ch
+            sign = -1.0 if ch == 3 else 1.0
+            base = PAD + r * 32
+            for j in range(4):
+                plain = m_halo[0, r // 2, ch, pl.ds(take + j, 1), :]
+                pole = sign * m_halo[0, r // 2, turned, pl.ds(take + 3 - j, 1), :]
+                mh[ch, pl.ds(base + j, 1), :] = jnp.where(at_south, pole, plain)
+                plain = m_halo[1, r // 2, ch, pl.ds(take + j, 1), :]
+                pole = sign * m_halo[1, r // 2, turned, pl.ds(take + 3 - j, 1), :]
+                mh[ch, pl.ds(base + 24 + j, 1), :] = jnp.where(at_north, pole, plain)
+            mh[ch, pl.ds(base + 4, 12), :] = ms[ch * 4 + r, pl.ds(PAD, 12), :]
+            mh[ch, pl.ds(base + 16, 8), :] = ms[ch * 4 + r, pl.ds(PAD + cells - 8, 8), :]
+            mh[ch, pl.ds(base + 28, 4), :] = jnp.zeros((4, 128), F32)
+    advance_strips(mh, mh1, products, weights, rows_dev)
+    advance(ms2, ms1, ms, products, weights, cells, rows_dev, None)
     part_left.wait()
     part_right.wait()
     for r in range(rows_dev):
@@ -368,19 +366,22 @@
 
 def finish(
     cells, rows_dev,
-    zs, ms, ms1, mh, mh1, weights, co_in,
+    zs, ms, ms1, mh, weights, co_in,
     zo_hbm, mo_hbm, co_hbm,
-    zo, mo, products, sems,
+    zo, mo, ms2, products, sems,
 ):
     co_copy = pltpu.make_async_copy(co_in, co_hbm, sems.at[2])
     co_copy.start()
     store_state(zo, zs, cells, rows_dev)
     zo_copy = pltpu.make_async_copy(zo, zo_hbm, sems.at[0])
     zo_copy.start()
-    substep(
-        (ms, ms1), (mh, mh1), products, weights, (SUB - 1) % 2, SUB % 2, cells, rows_dev, None, False
-    )
-    store_state(mo, ms, cells, rows_dev)
+    advance(ms1, ms2, ms, products, weights, cells, rows_dev, None)
+    for r in range(rows_dev):
+        for w in range(3):
+            at, base = w * 4 + r, PAD + r * 32
+            ms2[at, pl.ds(PAD, 4), :] = mh[w, pl.ds(base + 4, 4), :]
+            ms2[at, pl.ds(PAD + cells - 4, 4), :] = mh[w, pl.ds(base + 20, 4), :]
+    store_state(mo, ms2, cells, rows_dev)
     mo_copy = pltpu.make_async_copy(mo, mo_hbm, sems.at[1])
     mo_copy.start()
     co_copy.wait()
@@ -400,21 +401,21 @@
         hbm = pl.BlockSpec(memory_space=pltpu.HBM)
         shape = jax.ShapeDtypeStruct
         state = (16, cells + 2 * PAD, 128)
-        strips = (4, 16 * rows_dev + 2 * PAD, 128)
+        strips = (4, 32 * rows_dev + 2 * PAD, 128)
         packet = pltpu.VMEM((2, 4, 8, 128), F32)
         small = pltpu.VMEM((8, 128), F32)
-        products = pltpu.VMEM((rows_dev * 3 * cells + 3 * 16 * rows_dev, 128), F32)
+        products = pltpu.VMEM((rows_dev * 3 * cells, 128), F32)
         dma = pltpu.SemaphoreType.DMA
         held = pl.pallas_call(
             functools.partial(kernel, n, n_lat, cells, rows_dev),
             out_shape=(
                 shape(state, F32), shape(state, F32), shape(state, F32),
-                shape(strips, F32), shape(strips, F32),
+                shape(strips, F32),
                 shape((256, 256), jnp.bfloat16),
                 shape((GLON_DEV, rows_dev, nv * lev), F32),
             ),
             in_specs=[hbm] * 7,
-            out_specs=(vmem,) * 7,
+            out_specs=(vmem,) * 6,
             scratch_shapes=[
                 pltpu.SMEM((rows_dev,), jnp.int32),
                 pltpu.VMEM((flat, cells), F32),
@@ -424,15 +425,15 @@
                 pltpu.VMEM((lev * rows_dev, cells), F32),
                 pltpu.VMEM((nv * lev, lev), F32),
                 dma((7,)),
-                pltpu.VMEM(state, F32), pltpu.VMEM(strips, F32), pltpu.VMEM(strips, F32),
+                pltpu.VMEM(state, F32), pltpu.VMEM(state, F32), pltpu.VMEM(state, F32),
+                pltpu.VMEM(strips, F32), pltpu.VMEM(strips, F32), pltpu.VMEM(strips, F32),
                 products,
-                pltpu.VMEM((rows_dev, cells, 128), F32),
                 packet, packet, packet, packet, packet,
                 packet, packet, packet,
                 pltpu.VMEM((n, 4, 8, 128), F32),
                 pltpu.VMEM((4, 8, 128), F32),
                 pltpu.VMEM((2, 2, 4, 8, 128), F32),
-                pltpu.VMEM((rows_dev, 4, 32, 128), F32),
+                pltpu.VMEM((rows_dev, 4, 40, 128), F32),
                 small, small, small, small,
                 dma((8,)), dma((9,)), dma((1,)), dma((n,)), dma((n,)),
             ],
@@ -459,10 +460,11 @@
                 shape((flat, cells), F32), shape((flat, cells), F32),
                 shape((GLON_DEV, rows_dev, nv * lev), F32),
             ),
-            in_specs=[vmem] * 7,
+            in_specs=[vmem] * 6,
             out_specs=(hbm,) * 3,
             scratch_shapes=[
-                pltpu.VMEM((flat, cells), F32), pltpu.VMEM((flat, cells), F32), products, dma((3,)),
+                pltpu.VMEM((flat, cells), F32), pltpu.VMEM((flat, cells), F32),
+                pltpu.VMEM(state, F32), products, dma((3,)),
             ],
             compiler_params=pltpu.CompilerParams(vmem_limit_bytes=40 * 1024 * 1024),
         )(*held)

time: 21.2 us -> 19.7 us (0.929)
  Pallas kernels: 20.4 us -> 18.9 us
    pallas_call x1, Pallas kernels: 18.9 us -> 17.3 us  [shards(): pl.pallas_call(functools.partial(kernel, n, n_lat, cells, rows_dev), out_...]
where the time goes in v3:
time: 19.7 us; the launch traced here: 19.6 us
  Pallas kernels  18.9 us (96%)
  between operations  0.64 us (3%)
    pallas_call x1, Pallas kernels, shards(): pl.pallas_call(functools.partial(kernel, n, n_lat, cells, rows_dev), out_...  17.3 us
    pallas_call x1, Pallas kernels, shards(): pl.pallas_call(functools.partial(finish, cells, rows_dev), out_shape=(sha...  1.61 us

profile of v3, /device:TPU:0, one launch (start us, length us, event | category | flops | bytes accessed | tf_op | source)
XLA Modules:
  0.0 19.6 jit_solution(18393157683939726459)
XLA Ops:
  0.6 17.3 %shard_map.94 = (f32[16,144,128]{2,1,0:T(8,128)S(1)}, f32[16,144,128]{2,1,0:T(8,128)S(1)}, f32[16,144,128]{2,1,0:T(8,128)S(1)}, f32[4,144,128]{2,1,0:T(8,128)S(1...) custom-call(s32[4]{0:T(128)} %len_hbm.1, f32[1536,128]{1,0:T(8,128)} %bitcast.7, f32[128,128]{1,0:T(8,128)} %bitcast.9, ...), custom_call_target="tpu_custom_call" | custom-call | tf_op jit(solution)/shard_map/pallas_call | solution.py:409
  17.9 1.6 %shard_map.95 = (f32[1536,128]{1,0:T(8,128)}, f32[1536,128]{1,0:T(8,128)}, f32[4,4,128]{2,1,0:T(4,128)}) custom-call(f32[16,144,128]{2,1,0:T(8,128)S(1)} %get-tuple-element.12.zs, f32[16,144,128]{2,1,0:T(8,128)S(1)} %get-tuple-element.13.ms, f32[16,144,128]{2,1,0:T(8,128)S(1)} %get-tuple-element.14.ms1, f32[4,144,128]{2,1,0:T(8,128)S(1)} %get-tuple-element.15.mh, ...), custom_call_target="tpu_custom_call" | custom-call | tf_op jit(solution)/shard_map/pallas_call | solution.py:457
